TPU v7x, 32 devices: a whole 2x2x4 slice. The times are simulated.
32 devices in a mesh: dp: 16 (over z, y, x), tensor: 2 (over core).
Axes of the slice: x: 2, y: 2, z: 4, core: 2. Of those that a mesh axis runs over, the one named last changes fastest.
Arguments:
- tokens: bfloat16 [16384, 768], P('dp'), may hold values from -6 to 6
- memory: bfloat16 [16384, 768], P('dp'), may hold values from -6 to 6
- segment: int32 [16384], P('dp'), may hold values from 0 to 3, as said below
- cotangent: bfloat16 [16384, 768], P('dp'), may hold values from -6 to 6
- self_query: bfloat16 [768, 768], P(None, 'tensor'), may hold values from -0.21875 to 0.21875
- self_query_bias: bfloat16 [768], P('tensor'), may hold values from -3 to 3
- self_key: bfloat16 [768, 768], P(None, 'tensor'), may hold values from -0.21875 to 0.21875
- self_value: bfloat16 [768, 768], P(None, 'tensor'), may hold values from -0.21875 to 0.21875
- self_value_bias: bfloat16 [768], P('tensor'), may hold values from -3 to 3
- self_output: bfloat16 [768, 768], P('tensor'), may hold values from -0.75 to 0.75
- self_output_bias: bfloat16 [768], replicated, may hold values from -3 to 3
- cross_query: bfloat16 [768, 768], P(None, 'tensor'), may hold values from -0.21875 to 0.21875
- cross_query_bias: bfloat16 [768], P('tensor'), may hold values from -3 to 3
- cross_key: bfloat16 [768, 768], P(None, 'tensor'), may hold values from -0.21875 to 0.21875
- cross_value: bfloat16 [768, 768], P(None, 'tensor'), may hold values from -0.21875 to 0.21875
- cross_value_bias: bfloat16 [768], P('tensor'), may hold values from -3 to 3
- cross_output: bfloat16 [768, 768], P('tensor'), may hold values from -0.75 to 0.75
- cross_output_bias: bfloat16 [768], replicated, may hold values from -3 to 3
- first_gain: bfloat16 [768], replicated, may hold values from 0.5 to 1.5
- first_shift: bfloat16 [768], replicated, may hold values from -3 to 3
- second_gain: bfloat16 [768], replicated, may hold values from 0.5 to 1.5
- second_shift: bfloat16 [768], replicated, may hold values from -3 to 3
- third_gain: bfloat16 [768], replicated, may hold values from 0.5 to 1.5
- third_shift: bfloat16 [768], replicated, may hold values from -3 to 3
- inner_weight: bfloat16 [768, 3072], P(None, 'tensor'), may hold values from -0.21875 to 0.21875
- inner_bias: bfloat16 [3072], P('tensor'), may hold values from -3 to 3
- outer_weight: bfloat16 [3072, 768], P('tensor'), may hold values from -0.21875 to 0.21875
- outer_bias: bfloat16 [768], replicated, may hold values from -3 to 3
Outputs:
- output: bfloat16 [16384, 768], P('dp')
- grad_tokens: float32 [16384, 768], P(('dp', 'tensor'))
- grad_memory: float32 [16384, 768], P(('dp', 'tensor'))
- grad_self_query: float32 [768, 768], P('dp', 'tensor')
- grad_self_query_bias: float32 [768], P('tensor')
- grad_self_key: float32 [768, 768], P('dp', 'tensor')
- grad_self_value: float32 [768, 768], P('dp', 'tensor')
- grad_self_value_bias: float32 [768], P('tensor')
- grad_self_output: float32 [768, 768], P('tensor', 'dp')
- grad_self_output_bias: float32 [768], replicated
- grad_cross_query: float32 [768, 768], P('dp', 'tensor')
- grad_cross_query_bias: float32 [768], P('tensor')
- grad_cross_key: float32 [768, 768], P('dp', 'tensor')
- grad_cross_value: float32 [768, 768], P('dp', 'tensor')
- grad_cross_value_bias: float32 [768], P('tensor')
- grad_cross_output: float32 [768, 768], P('tensor', 'dp')
- grad_cross_output_bias: float32 [768], replicated
- grad_first_gain: float32 [768], replicated
- grad_first_shift: float32 [768], replicated
- grad_second_gain: float32 [768], replicated
- grad_second_shift: float32 [768], replicated
- grad_third_gain: float32 [768], replicated
- grad_third_shift: float32 [768], replicated
- grad_inner_weight: float32 [768, 3072], P('dp', 'tensor')
- grad_inner_bias: float32 [3072], P('tensor')
- grad_outer_weight: float32 [3072, 768], P('tensor', 'dp')
- grad_outer_bias: float32 [768], replicated
Inputs may be any that keep to these rules, and one draw needn't show every extreme that they name: Within each block of 1024 consecutive positions the segment is either 0 throughout (one long row) or position // 256 (four rows of 256); half of the blocks are of each kind.
All inputs are finite; a program needn't handle non-finite values.
Results may differ from a plain program's by a relative error of at most 0.028.
Values may be sent and summed in bfloat16 or wider, within the bound.
A program may use at most 256 MiB of HBM per device.

v0:
```python
from functools import partial

import jax
import jax.numpy as jnp
from jax import lax
from jax.sharding import PartitionSpec as P

HD = 64


EPSILON = 1e-05
NEGATIVE = -1e30


def normalize(hidden, gain, shift):
    center = hidden - jnp.mean(hidden, -1, keepdims=True)
    spread = jnp.mean(center * center, -1, keepdims=True)
    return center * lax.rsqrt(spread + EPSILON) * gain + shift


def project(data, weight):
    return jnp.dot(data, weight, preferred_element_type=jnp.float32)


def column_sums(values):
    return jnp.sum(values.astype(jnp.float32), 0)


def heads_of(matrix):
    return matrix.reshape(matrix.shape[0], -1, HD)


def allowed_pairs(query_segment, key_segment, start, causal):
    same = query_segment[:, None] == key_segment[None, :]
    if causal:
        query_place = start + jnp.arange(query_segment.shape[0], dtype=jnp.int32)
        key_place = jnp.arange(key_segment.shape[0], dtype=jnp.int32)
        same = same & (key_place[None, :] <= query_place[:, None])
    return same[None]


def attend_forward(queries, keys, values, segment, causal):
    length = queries.shape[0]
    block_rows = min(256 if causal else 512, length)
    contexts = []
    totals = []
    for index in range(length // block_rows):
        start = index * block_rows
        end = start + block_rows if causal else length
        piece = queries[start : start + block_rows]
        scores = jnp.einsum(
            "qhe,khe->hqk", piece, keys[:end], preferred_element_type=jnp.float32
        )
        scores = jnp.where(
            allowed_pairs(segment[start : start + block_rows], segment[:end], start, causal),
            scores,
            NEGATIVE,
        )
        highest = jnp.max(scores, -1, keepdims=True)
        powers = jnp.exp(scores - highest)
        summed = jnp.sum(powers, -1, keepdims=True)
        weights = (powers / summed).astype(jnp.bfloat16)
        contexts.append(
            jnp.einsum("hqk,khe->qhe", weights, values[:end], preferred_element_type=jnp.float32)
        )
        totals.append(highest + jnp.log(summed))
    return (jnp.concatenate(contexts, 0), jnp.concatenate(totals, 1))


def attend_backward(queries, keys, values, grad_context, totals, segment, causal):
    length = queries.shape[0]
    block_rows = min(256 if causal else 512, length)
    grad_queries = []
    grad_keys = jnp.zeros(keys.shape, jnp.float32)
    grad_values = jnp.zeros(values.shape, jnp.float32)
    for index in range(length // block_rows):
        start = index * block_rows
        end = start + block_rows if causal else length
        piece = queries[start : start + block_rows]
        grad_piece = grad_context[start : start + block_rows]
        near_keys = keys[:end]
        scores = jnp.einsum("qhe,khe->hqk", piece, near_keys, preferred_element_type=jnp.float32)
        scores = jnp.where(
            allowed_pairs(segment[start : start + block_rows], segment[:end], start, causal),
            scores,
            NEGATIVE,
        )
        probs = jnp.exp(scores - totals[:, start : start + block_rows])
        grad_probs = jnp.einsum(
            "qhe,khe->hqk", grad_piece, values[:end], preferred_element_type=jnp.float32
        )
        row_inner = jnp.sum(grad_probs * probs, -1, keepdims=True)
        grad_scores = (probs * (grad_probs - row_inner)).astype(jnp.bfloat16)
        grad_queries.append(
            jnp.einsum("hqk,khe->qhe", grad_scores, near_keys, preferred_element_type=jnp.float32)
        )
        grad_keys = grad_keys.at[:end].add(
            jnp.einsum("hqk,qhe->khe", grad_scores, piece, preferred_element_type=jnp.float32)
        )
        grad_values = grad_values.at[:end].add(
            jnp.einsum(
                "hqk,qhe->khe",
                probs.astype(jnp.bfloat16),
                grad_piece,
                preferred_element_type=jnp.float32,
            )
        )
    return (jnp.concatenate(grad_queries, 0), grad_keys, grad_values)


def on_device(
    tokens,
    memory,
    segment,
    cotangent,
    self_query,
    self_query_bias,
    self_key,
    self_value,
    self_value_bias,
    self_output,
    self_output_bias,
    cross_query,
    cross_query_bias,
    cross_key,
    cross_value,
    cross_value_bias,
    cross_output,
    cross_output_bias,
    first_gain,
    first_shift,
    second_gain,
    second_shift,
    third_gain,
    third_shift,
    inner_weight,
    inner_bias,
    outer_weight,
    outer_bias,
):
    scale = HD ** (-0.5)
    length = tokens.shape[0]
    groups = lax.axis_size("tensor")
    member = lax.axis_index("tensor")
    half = length // groups

    def rows_of(values):
        return lax.dynamic_slice_in_dim(values, member * half, half, 0)

    def spread_out(values):
        whole = jnp.zeros((values.shape[0] * groups,), jnp.float32)
        return lax.dynamic_update_slice_in_dim(whole, values, member * values.shape[0], 0)

    def own_share(values, count):
        return lax.dynamic_slice_in_dim(values, member * count, count, 0)

    def swap(values):
        return lax.ppermute(values, "tensor", [(0, 1), (1, 0)])

    def gather_rows(values):
        if groups != 2:
            return lax.all_gather(values, "tensor", axis=0, tiled=True)
        other = swap(values)
        lead = member == 0
        return jnp.concatenate(
            [jnp.where(lead, values, other), jnp.where(lead, other, values)], 0
        )

    def scatter_rows(values):
        if groups != 2:
            return lax.psum_scatter(
                values, "tensor", scatter_dimension=0, tiled=True
            ).astype(jnp.float32)
        top = values[:half]
        bottom = values[half:]
        lead = member == 0
        keep = jnp.where(lead, top, bottom)
        send = jnp.where(lead, bottom, top)
        return keep.astype(jnp.float32) + swap(send).astype(jnp.float32)

    def sum_pair(values):
        if groups != 2:
            return lax.psum(values, "tensor").astype(jnp.float32)
        return values.astype(jnp.float32) + swap(values).astype(jnp.float32)

    queries = ((project(tokens, self_query) + self_query_bias.astype(jnp.float32)) * scale).astype(
        jnp.bfloat16
    )
    keys = project(tokens, self_key).astype(jnp.bfloat16)
    values = (project(tokens, self_value) + self_value_bias.astype(jnp.float32)).astype(
        jnp.bfloat16
    )
    self_queries = heads_of(queries)
    self_keys = heads_of(keys)
    self_values = heads_of(values)
    self_context, self_totals = attend_forward(self_queries, self_keys, self_values, segment, True)
    self_context = self_context.reshape(length, -1).astype(jnp.bfloat16)
    attended = scatter_rows(project(self_context, self_output)) + self_output_bias.astype(
        jnp.float32
    )
    first, first_back = jax.vjp(
        normalize,
        rows_of(tokens).astype(jnp.float32) + attended,
        first_gain.astype(jnp.float32),
        first_shift.astype(jnp.float32),
    )
    first_low = gather_rows(first.astype(jnp.bfloat16))
    queries = (
        (project(first_low, cross_query) + cross_query_bias.astype(jnp.float32)) * scale
    ).astype(jnp.bfloat16)
    keys = project(memory, cross_key).astype(jnp.bfloat16)
    values = (project(memory, cross_value) + cross_value_bias.astype(jnp.float32)).astype(
        jnp.bfloat16
    )
    cross_queries = heads_of(queries)
    cross_keys = heads_of(keys)
    cross_values = heads_of(values)
    cross_context, cross_totals = attend_forward(
        cross_queries, cross_keys, cross_values, segment, False
    )
    cross_context = cross_context.reshape(length, -1).astype(jnp.bfloat16)
    crossed = scatter_rows(
        project(cross_context, cross_output).astype(jnp.bfloat16)
    ) + cross_output_bias.astype(jnp.float32)
    second_part, second_back = jax.vjp(
        normalize,
        first + crossed,
        second_gain.astype(jnp.float32),
        second_shift.astype(jnp.float32),
    )
    second = gather_rows(second_part.astype(jnp.bfloat16)).astype(second_part.dtype)
    second_low = second.astype(jnp.bfloat16)
    inner = project(second_low, inner_weight) + inner_bias.astype(jnp.float32)
    hidden = jax.nn.gelu(inner, approximate=False).astype(jnp.bfloat16)
    outer = sum_pair(project(hidden, outer_weight).astype(jnp.bfloat16)) + outer_bias.astype(
        jnp.float32
    )
    result, third_back = jax.vjp(
        normalize, second + outer, third_gain.astype(jnp.float32), third_shift.astype(jnp.float32)
    )
    output = result.astype(jnp.bfloat16)
    grad_third, grad_third_gain, grad_third_shift = third_back(cotangent.astype(jnp.float32))
    grad_outer = grad_third.astype(jnp.bfloat16)
    grad_outer_bias = column_sums(grad_outer)
    gelu_back = jax.vjp(partial(jax.nn.gelu, approximate=False), inner)[1]
    grad_inner = gelu_back(project(grad_outer, outer_weight.T))[0].astype(jnp.bfloat16)
    grad_inner_weight = project(second_low.T, grad_inner)
    grad_inner_bias = column_sums(grad_inner)
    grad_second = rows_of(grad_third) + scatter_rows(
        project(grad_inner, inner_weight.T).astype(jnp.bfloat16)
    )
    grad_second_in, grad_second_gain, grad_second_shift = second_back(grad_second)
    grad_cross_rows = grad_second_in.astype(jnp.bfloat16)
    grad_cross = gather_rows(grad_cross_rows)
    grad_cross_output_bias = column_sums(grad_cross)
    grad_cross_context = heads_of(project(grad_cross, cross_output.T).astype(jnp.bfloat16))
    cross_grad_q, cross_grad_k, cross_grad_v = attend_backward(
        cross_queries, cross_keys, cross_values, grad_cross_context, cross_totals, segment, False
    )
    cross_grad_q = (cross_grad_q.astype(jnp.bfloat16) * scale).reshape(length, -1)
    cross_grad_k = cross_grad_k.astype(jnp.bfloat16).reshape(length, -1)
    cross_grad_v = cross_grad_v.astype(jnp.bfloat16).reshape(length, -1)
    grad_cross_query = project(first_low.T, cross_grad_q)
    grad_cross_query_bias = column_sums(cross_grad_q)
    grad_cross_key = project(memory.T, cross_grad_k)
    grad_cross_value = project(memory.T, cross_grad_v)
    grad_cross_value_bias = column_sums(cross_grad_v)
    memory_term = project(cross_grad_k, cross_key.T) + project(cross_grad_v, cross_value.T)
    grad_first = grad_second_in + scatter_rows(
        project(cross_grad_q, cross_query.T).astype(jnp.bfloat16)
    )
    grad_first_in, grad_first_gain, grad_first_shift = first_back(grad_first)
    grad_self_rows = grad_first_in.astype(jnp.bfloat16)
    grad_self = gather_rows(grad_self_rows)
    grad_self_output_bias = column_sums(grad_self)
    grad_self_context = heads_of(project(grad_self, self_output.T).astype(jnp.bfloat16))
    dp_size = lax.axis_size("dp")
    grad_cross_output_t = project(grad_cross.T, cross_context)
    cross = [grad_cross_query, grad_cross_key, grad_cross_value, grad_cross_output_t]
    cross_joined = jnp.concatenate(cross, 1).astype(jnp.bfloat16)
    cross_joined, grad_self_context = lax.optimization_barrier((cross_joined, grad_self_context))
    self_grad_q, self_grad_k, self_grad_v = attend_backward(
        self_queries, self_keys, self_values, grad_self_context, self_totals, segment, True
    )
    self_grad_q = (self_grad_q.astype(jnp.bfloat16) * scale).reshape(length, -1)
    self_grad_k = self_grad_k.astype(jnp.bfloat16).reshape(length, -1)
    self_grad_v = self_grad_v.astype(jnp.bfloat16).reshape(length, -1)
    grad_self_query = project(tokens.T, self_grad_q)
    grad_self_query_bias = column_sums(self_grad_q)
    grad_self_key = project(tokens.T, self_grad_k)
    grad_self_value = project(tokens.T, self_grad_v)
    grad_self_value_bias = column_sums(self_grad_v)
    tokens_term = (
        project(self_grad_q, self_query.T)
        + project(self_grad_k, self_key.T)
        + project(self_grad_v, self_value.T)
    )
    tokens_part = scatter_rows(tokens_term.astype(jnp.bfloat16))
    memory_part = scatter_rows(memory_term.astype(jnp.bfloat16))
    grad_tokens = tokens_part + grad_first_in
    grad_self_output_t = project(grad_self.T, self_context)
    grad_outer_weight_t = project(grad_outer.T, hidden)

    def split_columns(summed, pieces, flipped):
        parts = []
        offset = 0
        for position, piece in enumerate(pieces):
            width = piece.shape[1]
            part = summed[:, offset : offset + width]
            offset += width
            if position in flipped:
                part = part.T
            parts.append(part)
        return parts

    def exchange_sum(joined, extra=None):
        rows = joined.shape[0] // dp_size
        blocks = joined.reshape(dp_size, rows, joined.shape[1])
        if extra is not None:
            blocks = jnp.concatenate(
                [blocks, jnp.broadcast_to(extra[None], (dp_size,) + extra.shape)], 1
            )
        received = lax.all_to_all(blocks, "dp", 0, 0, tiled=True)
        return jnp.sum(received.astype(jnp.float32), 0)

    ffn = [grad_inner_weight, grad_outer_weight_t]
    ffn_sum = lax.psum_scatter(
        jnp.concatenate(ffn, 1).astype(jnp.bfloat16), "dp", scatter_dimension=0, tiled=True
    ).astype(jnp.float32)
    ffn_sums = split_columns(ffn_sum, ffn, (1,))
    cross_sums = split_columns(exchange_sum(cross_joined), cross, (3,))
    late = [grad_self_query, grad_self_key, grad_self_value, grad_self_output_t]
    late_joined = jnp.concatenate(late, 1).astype(jnp.bfloat16)
    norm_pairs = sum_pair(
        jnp.concatenate([grad_first_gain, grad_first_shift, grad_second_gain, grad_second_shift])
    )
    vector = jnp.concatenate(
        [
            grad_self_query_bias,
            grad_self_value_bias,
            grad_self_output_bias,
            grad_cross_query_bias,
            grad_cross_value_bias,
            grad_cross_output_bias,
            norm_pairs,
            grad_third_gain,
            grad_third_shift,
            grad_inner_bias,
            grad_outer_bias,
        ]
    )
    width = late_joined.shape[1]
    lines = -(-vector.shape[0] // width)
    padded = jnp.pad(vector, (0, lines * width - vector.shape[0])).reshape(lines, width)
    high = padded.astype(jnp.bfloat16)
    low = (padded - high.astype(jnp.float32)).astype(jnp.bfloat16)
    late_rows = late_joined.shape[0] // dp_size
    late_total = exchange_sum(late_joined, jnp.concatenate([high, low], 0))
    self_sums = split_columns(late_total[:late_rows], late, (3,))
    total = (
        late_total[late_rows : late_rows + lines] + late_total[late_rows + lines :]
    ).reshape(-1)
    smalls = []
    offset = 0
    for piece in (
        grad_self_query_bias,
        grad_self_value_bias,
        grad_self_output_bias,
        grad_cross_query_bias,
        grad_cross_value_bias,
        grad_cross_output_bias,
        grad_first_gain,
        grad_first_shift,
        grad_second_gain,
        grad_second_shift,
        grad_third_gain,
        grad_third_shift,
        grad_inner_bias,
        grad_outer_bias,
    ):
        smalls.append(total[offset : offset + piece.shape[0]])
        offset += piece.shape[0]
    return (
        output,
        grad_tokens,
        memory_part,
        self_sums[0],
        smalls[0],
        self_sums[1],
        self_sums[2],
        smalls[1],
        self_sums[3],
        smalls[2],
        cross_sums[0],
        smalls[3],
        cross_sums[1],
        cross_sums[2],
        smalls[4],
        cross_sums[3],
        smalls[5],
        smalls[6],
        smalls[7],
        smalls[8],
        smalls[9],
        smalls[10],
        smalls[11],
        ffn_sums[0],
        smalls[12],
        ffn_sums[1],
        smalls[13],
    )


def solution(mesh):
    return jax.shard_map(
        on_device,
        mesh=mesh,
        in_specs=(
            P("dp", None),
            P("dp", None),
            P("dp"),
            P("dp", None),
            P(None, "tensor"),
            P("tensor"),
            P(None, "tensor"),
            P(None, "tensor"),
            P("tensor"),
            P("tensor", None),
            P(),
            P(None, "tensor"),
            P("tensor"),
            P(None, "tensor"),
            P(None, "tensor"),
            P("tensor"),
            P("tensor", None),
            P(),
            P(),
            P(),
            P(),
            P(),
            P(),
            P(),
            P(None, "tensor"),
            P("tensor"),
            P("tensor", None),
            P(),
        ),
        out_specs=(
            P("dp", None),
            P(("dp", "tensor"), None),
            P(("dp", "tensor"), None),
            P("dp", "tensor"),
            P("tensor"),
            P("dp", "tensor"),
            P("dp", "tensor"),
            P("tensor"),
            P("tensor", "dp"),
            P(),
            P("dp", "tensor"),
            P("tensor"),
            P("dp", "tensor"),
            P("dp", "tensor"),
            P("tensor"),
            P("tensor", "dp"),
            P(),
            P(),
            P(),
            P(),
            P(),
            P(),
            P(),
            P("dp", "tensor"),
            P("tensor"),
            P("tensor", "dp"),
            P(),
        ),
        check_vma=False,
    )
```

profile of v0, /device:TPU:12, one launch (start us, length us, event | category | flops | bytes accessed | tf_op | source)
XLA Modules:
  0.0 425.8 jit_solution(15335810624817632143)
XLA Ops:
  12.4 2.5 add_convert_fusion.8
  21.5 2.4 multiply_convert_fusion.8
  40.5 2.3 fusion.92
  50.9 2.9 fusion.153
  59.4 2.1 select_reduce_fusion
  61.6 3.4 fusion.1
  66.1 4.5 %fusion.88 = bf16[512,6,64]{0,2,1:T(8,128)(2,1)S(1)} fusion(bf16[1024,6,64]{0,2,1:T(8,128)(2,1)S(1)} %bitcast.261, f32[6,512,1024]{2,1,0:T(8,128)S(1)} %get-tuple-element.363, f32[6,512]{1,0:T(8,128)S(1)} %fusion.1, f32[6,512]{1,0:T(8,128)S(1)} %get-tuple-element.362, pred[512,1024]{1,0:T(8,128)(4,1)S(1)} %get-tuple-element.347), kind=kOutput, calls=%fused_computation.192 | convolution fusion | flops 415432704 | bytes 14311424 | tf_op jit(solution)/shard_map/hqk,khe->qhe/dot_general | solution.py:64
  70.7 2.1 select_reduce_fusion.1
  72.8 3.4 fusion
  77.4 4.1 fusion.87
  83.1 2.1 collective-permute-done.2
  86.7 2.1 collective-permute-done.3
  89.3 18.2 %multiply_convert_fusion.3 = (bf16[1024,1536]{1,0:T(8,128)(2,1)S(1)}, f32[1024,1536]{1,0:T(8,128)}, f32[1024,1536]{1,0:T(8,128)}) fusion(f32[1536]{0:T(1024)S(1)} %convert_element_type.331, bf16[768,1536]{1,0:T(8,128)(2,1)S(1)} %copy-done, bf16[512,768]{0,1:T(8,128)(2,1)S(1)} %get-tuple-element.312, bf16[512,768]{0,1:T(8,128)(2,1)S(1)} %get-tuple-element.311), kind=kOutput, calls=%fused_computation.28 | convolution fusion | flops 2522873856 | bytes 19666944 | tf_op jit(solution)/shard_map/dot_general | solution.py:22
  107.6 3.8 convolution_convert_fusion.5
  112.2 1.7 copy.98
  113.9 2.7 copy.84
  116.6 1.7 copy.99
  118.4 1.7 copy.100
  120.1 1.8 copy.101
  123.3 3.2 fusion.150
  128.2 2.2 fusion.30
  130.4 3.2 convert_reduce_fusion.4
  133.6 7.5 %convert_reduce_fusion.1 = (f32[1536]{0:T(1024)}, bf16[1024,1536]{1,0:T(8,128)(2,1)S(1)}) fusion(f32[1024,1536]{1,0:T(8,128)S(1)} %bitcast.329, bf16[1536,768]{1,0:T(8,128)(2,1)S(1)} %copy-done.168, f32[1024,768]{0,1:T(8,128)S(1)} %get-tuple-element.291, f32[1024,1536]{1,0:T(8,128)} %get-tuple-element.366, f32[1536]{0:T(1024)S(1)} %copy-done.151), kind=kOutput, calls=%fused_computation.21 | convolution fusion | flops 2443442688 | bytes 21245952 | tf_op jit(solution)/shard_map/dot_general | solution.py:22
  141.1 2.6 convolution_convert_fusion.4
  144.3 2.8 convolution_convert_fusion
  151.1 3.0 convolution_convert_fusion.1
  154.1 2.7 pad_maximum_fusion
  162.1 6.6 %fusion.4 = f32[6,64,1024]{2,1,0:T(8,128)S(1)} fusion(bf16[512,6,64]{0,2,1:T(8,128)(2,1)S(1)} %bitcast.259, f32[6,512,1024]{2,1,0:T(8,128)} %copy-done.3, f32[6,512]{1,0:T(8,128)S(1)} %log_add_fusion, pred[512,1024]{1,0:T(8,128)(4,1)S(1)} %get-tuple-element.347), kind=kOutput, calls=%fused_computation.17 | convolution fusion | flops 412090368 | bytes 15085568 | tf_op jit(solution)/shard_map/hqk,qhe->khe/dot_general | solution.py:101
  168.7 9.8 %multiply_reduce_fusion = (f32[6,512]{1,0:T(8,128)S(1)}, f32[6,512,1024]{2,1,0:T(8,128)}) fusion(f32[6,512,1024]{2,1,0:T(8,128)} %copy-done.3, f32[6,512]{1,0:T(8,128)S(1)} %log_add_fusion, pred[512,1024]{1,0:T(8,128)(4,1)S(1)} %get-tuple-element.347, bf16[512,6,64]{0,2,1:T(8,128)(2,1)S(1)} %bitcast.260, bf16[1024,6,64]{0,2,1:T(8,128)(2,1)S(1)} %bitcast.263), kind=kOutput, calls=%fused_computation.1 | convolution fusion | flops 415233024 | bytes 26894336 | tf_op jit(solution)/shard_map/qhe,khe->hqk/dot_general | solution.py:89
  178.5 7.2 %multiply_reduce_fusion.1 = (f32[6,512]{1,0:T(8,128)S(1)}, f32[6,512,1024]{2,1,0:T(8,128)}) fusion(f32[6,512,1024]{2,1,0:T(8,128)S(1)} %bitcast.225, f32[6,512]{1,0:T(8,128)S(1)} %log_add_fusion.1, pred[512,1024]{1,0:T(8,128)(4,1)S(1)} %get-tuple-element.346, bf16[512,6,64]{0,2,1:T(8,128)(2,1)S(1)} %bitcast.257, bf16[1024,6,64]{0,2,1:T(8,128)(2,1)S(1)} %bitcast.264), kind=kOutput, calls=%fused_computation.4 | convolution fusion | flops 415233024 | bytes 26894336 | tf_op jit(solution)/shard_map/qhe,khe->hqk/dot_general | solution.py:89
  185.6 18.5 %multiply_convert_fusion = (bf16[6,512,1024]{2,1,0:T(8,128)(2,1)}, bf16[6,512,1024]{2,1,0:T(8,128)(2,1)}) fusion(f32[6,512,1024]{2,1,0:T(8,128)} %get-tuple-element.370, f32[6,512,1024]{2,1,0:T(8,128)} %copy-done.3, f32[6,512]{1,0:T(8,128)S(1)} %get-tuple-element.369, f32[6,512]{1,0:T(8,128)S(1)} %log_add_fusion, pred[512,1024]{1,0:T(8,128)(4,1)S(1)} %get-tuple-element.347, ...), kind=kLoop, calls=%fused_computation | loop fusion | flops 31457280 | bytes 64012288 | tf_op jit(solution)/shard_map/convert_element_type | solution.py:93
  204.2 5.0 %convolution_convert_fusion.19 = bf16[6,64,512]{2,1,0:T(8,128)(2,1)S(1)} fusion(bf16[1024,6,64]{0,2,1:T(8,128)(2,1)S(1)} %bitcast.240, bf16[6,512,1024]{2,1,0:T(8,128)(2,1)} %get-tuple-element.386), kind=kOutput, calls=%fused_computation.186 | convolution fusion | flops 402849792 | bytes 7471104 | tf_op jit(solution)/shard_map/hqk,khe->qhe/dot_general | solution.py:95
  209.2 5.3 %fusion.163 = f32[6,64,1024]{2,1,0:T(8,128)} fusion(bf16[512,6,64]{0,2,1:T(8,128)(2,1)S(1)} %bitcast.252, bf16[6,512,1024]{2,1,0:T(8,128)(2,1)} %get-tuple-element.386), kind=kOutput, calls=%fused_computation.333 | convolution fusion | flops 402653184 | bytes 8257536 | tf_op jit(solution)/shard_map/hqk,qhe->khe/dot_general | solution.py:98
  214.6 2.1 convolution_convert_fusion.18
  219.3 4.9 %convert_reduce_fusion.7 = (f32[6,64]{1,0:T(8,128)S(1)}, bf16[6,64,1024]{2,1,0:T(8,128)(2,1)}) fusion(f32[6,64,1024]{2,1,0:T(8,128)S(1)} %fusion.4, bf16[512,6,64]{0,2,1:T(8,128)(2,1)S(1)} %bitcast.258, f32[6,512,1024]{2,1,0:T(8,128)S(1)} %bitcast.225, f32[6,512]{1,0:T(8,128)S(1)} %log_add_fusion.1, pred[512,1024]{1,0:T(8,128)(4,1)S(1)} %get-tuple-element.346), kind=kOutput, calls=%fused_computation.118 | convolution fusion | flops 413662848 | bytes 15873536 | tf_op jit(solution)/shard_map/hqk,qhe->khe/dot_general | solution.py:101
  225.9 2.4 fusion.81
  228.4 4.2 add_convert_fusion.5
  246.3 2.5 copy.102
  248.8 7.9 %all-to-all-start.1 = ((bf16[16,48,1536]{2,1,0:T(8,128)(2,1)}), bf16[16,48,1536]{2,1,0:T(8,128)(2,1)}, u32[]{:S(2)}, u32[]{:S(2)}) async-start(bf16[16,48,1536]{2,1,0:T(8,128)(2,1)} %bitcast.71), calls=%async_computation.1 | async-start | bytes 4718592 | tf_op jit(solution)/shard_map/all_to_all | solution.py:323
  256.8 5.1 %multiply_reduce_fusion.4 = (f32[6,256]{1,0:T(8,128)S(1)}, f32[6,256,512]{2,1,0:T(8,128)}) fusion(f32[6,256,512]{2,1,0:T(8,128)} %copy-done.6, f32[6,256]{1,0:T(8,128)S(1)} %log_add_fusion.4, pred[256,512]{1,0:T(8,128)(4,1)S(1)} %copy-done.48, bf16[512,6,64]{0,2,1:T(8,128)(2,1)S(1)} %bitcast.314, bf16[1024,6,64]{0,2,1:T(8,128)(2,1)S(1)} %bitcast.271), kind=kOutput, calls=%fused_computation.81 | convolution fusion | flops 103807488 | bytes 7026688 | tf_op jit(solution)/shard_map/qhe,khe->hqk/dot_general | solution.py:89
  264.1 3.6 multiply_reduce_fusion.3
  269.2 4.0 multiply_reduce_fusion.2
  273.2 2.4 convert_reduce_fusion.9
  276.3 3.4 multiply_convert_fusion.5
  280.9 3.6 multiply_convert_fusion.4
  286.8 1.8 multiply_convert_fusion.2
  290.1 1.9 constant_dynamic-update-slice_fusion.9
  300.1 2.2 copy.97
  302.3 2.3 scatter-add.20
  314.0 2.9 fusion.72
  316.9 3.0 fusion.66
  319.9 2.2 fusion.47
  323.5 3.2 fusion.82
  326.7 2.2 copy.95
  331.3 1.8 pad_maximum_fusion.1
  333.1 7.4 %all-to-all-start = ((bf16[16,62,1536]{2,1,0:T(8,128)(2,1)}), bf16[16,62,1536]{2,1,0:T(8,128)(2,1)}, u32[]{:S(2)}, u32[]{:S(2)}) async-start(bf16[16,62,1536]{2,1,0:T(8,128)(2,1)} %pad_maximum_fusion.1), calls=%async_computation | async-start | bytes 6291456 | tf_op jit(solution)/shard_map/all_to_all | solution.py:323
  348.4 2.6 copy.103
  351.0 3.2 convert_add_fusion
  354.2 3.0 copy.105
  357.2 3.0 add_add_fusion.4
  360.2 3.0 copy.104
  363.2 2.0 convert_reduce_fusion.3
  366.0 44.4 %all-to-all-done = bf16[16,62,1536]{2,1,0:T(8,128)(2,1)} async-done(((bf16[16,62,1536]{2,1,0:T(8,128)(2,1)}), bf16[16,62,1536]{2,1,0:T(8,128)(2,1)}, u32[]{:S(2)}, u32[]{:S(2)}) %all-to-all-start) | async-done | bytes 3047456 | tf_op jit(solution)/shard_map/all_to_all | solution.py:323
  410.3 2.4 convert_reduce_fusion
  (576 shorter events, 122.8 us)
Async XLA Ops:
  7.2 82.1 %copy-start = (bf16[768,1536]{1,0:T(8,128)(2,1)S(1)}, bf16[768,1536]{1,0:T(8,128)(2,1)}, u32[]{:S(2)}) copy-start(bf16[768,1536]{1,0:T(8,128)(2,1)} %param.88) | copy-start | bytes 7077892
  7.2 408.1 %reduce-scatter.2.cloned.1.call-start = ((), (), s32[]{:S(2)}) async-start(), calls=%async_computation.3 | async-start | bytes 5013504 | tf_op jit(solution)/shard_map/reduce_scatter | solution.py:327
  18.2 18.4 %copy-start.29 = (bf16[1024,384]{0,1:T(8,128)(2,1)}, bf16[1024,384]{0,1:T(8,128)(2,1)S(1)}, u32[]{:S(2)}) copy-start(bf16[1024,384]{0,1:T(8,128)(2,1)S(1)} %convolution_convert_fusion.9) | copy-start | bytes 2359300
  19.0 9.7 %copy-start.55 = (bf16[512,384]{0,1:T(8,128)(2,1)}, bf16[512,384]{0,1:T(8,128)(2,1)S(1)}, u32[]{:S(2)}) copy-start(bf16[512,384]{0,1:T(8,128)(2,1)S(1)} %slice.601) | copy-start | bytes 1179652
  25.8 13.7 %copy-start.31 = (pred[256,1024]{1,0:T(8,128)(4,1)}, pred[256,1024]{1,0:T(8,128)(4,1)S(1)}, u32[]{:S(2)}) copy-start(pred[256,1024]{1,0:T(8,128)(4,1)S(1)} %fusion.93) | copy-start | bytes 786436
  28.6 14.2 %copy-start.101 = (bf16[6,64,256]{2,1,0:T(8,128)(2,1)}, bf16[6,64,256]{2,1,0:T(8,128)(2,1)S(1)}, u32[]{:S(2)}) copy-start(bf16[6,64,256]{2,1,0:T(8,128)(2,1)S(1)} %convolution_convert_fusion.24) | copy-start | bytes 589828
  32.1 10.7 %copy-start.102 = (bf16[6,64,256]{2,1,0:T(8,128)(2,1)}, bf16[6,64,256]{2,1,0:T(8,128)(2,1)S(1)}, u32[]{:S(2)}) copy-start(bf16[6,64,256]{2,1,0:T(8,128)(2,1)S(1)} %fusion.91) | copy-start | bytes 589828
  36.6 6.2 %copy-start.103 = (bf16[6,64,256]{2,1,0:T(8,128)(2,1)}, bf16[6,64,256]{2,1,0:T(8,128)(2,1)S(1)}, u32[]{:S(2)}) copy-start(bf16[6,64,256]{2,1,0:T(8,128)(2,1)S(1)} %fusion.90) | copy-start | bytes 589828
  47.1 3.8 collective-permute-start
  47.2 38.0 %copy-start.125 = (f32[768]{0:T(1024)}, f32[768]{0:T(1024)S(1)}, u32[]{:S(2)}) copy-start(f32[768]{0:T(1024)S(1)} %convert_element_type.312) | copy-start | bytes 9220
  53.8 31.4 %copy-start.8 = (f32[512,768]{0,1:T(8,128)}, f32[512,768]{0,1:T(8,128)S(1)}, u32[]{:S(2)}) copy-start(f32[512,768]{0,1:T(8,128)S(1)} %get-tuple-element.305) | copy-start | bytes 4718596
  53.9 31.3 %copy-start.128 = (f32[512]{0:T(512)}, f32[512]{0:T(512)S(1)}, u32[]{:S(2)}) copy-start(f32[512]{0:T(512)S(1)} %broadcast_multiply_fusion.2) | copy-start | bytes 6148
  54.1 31.1 %copy-start.130 = (f32[512]{0:T(512)}, f32[512]{0:T(512)S(1)}, u32[]{:S(2)}) copy-start(f32[512]{0:T(512)S(1)} %fusion.120) | copy-start | bytes 6148
  54.5 3.3 collective-permute-start.1
  56.9 13.8 %copy-start.26 = (bf16[1024,384]{0,1:T(8,128)(2,1)}, bf16[1024,384]{0,1:T(8,128)(2,1)S(1)}, u32[]{:S(2)}) copy-start(bf16[1024,384]{0,1:T(8,128)(2,1)S(1)} %convolution_convert_fusion.8) | copy-start | bytes 2359300
  57.7 18.5 %copy-start.57 = (bf16[1024,384]{0,1:T(8,128)(2,1)}, bf16[1024,384]{0,1:T(8,128)(2,1)S(1)}, u32[]{:S(2)}) copy-start(bf16[1024,384]{0,1:T(8,128)(2,1)S(1)} %add_convert_fusion.7) | copy-start | bytes 2359300
  59.4 11.3 %copy-start.51 = (bf16[512,384]{0,1:T(8,128)(2,1)}, bf16[512,384]{0,1:T(8,128)(2,1)S(1)}, u32[]{:S(2)}) copy-start(bf16[512,384]{0,1:T(8,128)(2,1)S(1)} %get-tuple-element.317) | copy-start | bytes 1179652
  82.8 2.4 collective-permute-start.2
  86.5 2.4 collective-permute-start.3
  86.7 20.9 %copy-start.150 = (f32[1536]{0:T(1024)}, f32[1536]{0:T(1024)S(1)}, u32[]{:S(2)}) copy-start(f32[1536]{0:T(1024)S(1)} %convert_element_type.331) | copy-start | bytes 18436
  89.3 18.2 %copy-start.61 = (bf16[512,768]{0,1:T(8,128)(2,1)}, bf16[512,768]{0,1:T(8,128)(2,1)S(1)}, u32[]{:S(2)}) copy-start(bf16[512,768]{0,1:T(8,128)(2,1)S(1)} %get-tuple-element.311) | copy-start | bytes 2359300
  89.3 18.2 %copy-start.63 = (bf16[512,768]{0,1:T(8,128)(2,1)}, bf16[512,768]{0,1:T(8,128)(2,1)S(1)}, u32[]{:S(2)}) copy-start(bf16[512,768]{0,1:T(8,128)(2,1)S(1)} %get-tuple-element.312) | copy-start | bytes 2359300
  89.3 18.2 %copy-start.167 = (bf16[1536,768]{1,0:T(8,128)(2,1)S(1)}, bf16[1536,768]{1,0:T(8,128)(2,1)}, u32[]{:S(2)}) copy-start(bf16[1536,768]{1,0:T(8,128)(2,1)} %param.90) | copy-start | bytes 7077892
  111.4 10.5 %copy-start.133 = (f32[6,256]{1,0:T(8,128)S(1)}, f32[6,256]{1,0:T(8,128)}, u32[]{:S(2)}) copy-start(f32[6,256]{1,0:T(8,128)} %copy-done.132) | copy-start | bytes 18436
  111.4 10.5 %copy-start.137 = (f32[6,256]{1,0:T(8,128)S(1)}, f32[6,256]{1,0:T(8,128)}, u32[]{:S(2)}) copy-start(f32[6,256]{1,0:T(8,128)} %copy-done.136) | copy-start | bytes 18436
  111.4 11.9 %collective-permute-start.4 = (bf16[1024,768]{0,1:T(8,128)(2,1)}, bf16[1024,768]{0,1:T(8,128)(2,1)}, u32[]{:S(2)}, u32[]{:S(2)}) collective-permute-start(bf16[1024,768]{0,1:T(8,128)(2,1)} %convolution_convert_fusion.5), channel_id=1, source_target_pairs={{0,1},{1,0},{2,3},{3,2},{4,5},{5,4},{6,7},{7,6},{8,9},{9,8},{10,11... | collective-permute-start | bytes 4718600 | tf_op jit(solution)/shard_map/ppermute | solution.py:158
  126.5 7.1 %slice-start.15 = ((s8[6291456]{0:T(1024)(128)(4,1)}), s8[4194304]{0:T(1024)(128)(4,1)S(1)}, s32[]{:S(2)}) async-start(s8[6291456]{0:T(1024)(128)(4,1)} %bitcast.328), calls=%async_computation.19 | async-start | bytes 8388608
  143.9 3.3 collective-permute-start.5
  150.9 5.9 %collective-permute-start.6 = (bf16[512,768]{0,1:T(8,128)(2,1)}, bf16[512,768]{0,1:T(8,128)(2,1)}, u32[]{:S(2)}, u32[]{:S(2)}) collective-permute-start(bf16[512,768]{0,1:T(8,128)(2,1)} %add_convert_fusion.10), channel_id=1, source_target_pairs={{0,1},{1,0},{2,3},{3,2},{4,5},{5,4},{6,7},{7,6},{8,9},{9,8},{10,11... | collective-permute-start | bytes 2359304 | tf_op jit(solution)/shard_map/ppermute | solution.py:158
  162.1 6.6 %copy-start.58 = (bf16[1024,384]{0,1:T(8,128)(2,1)S(1)}, bf16[1024,384]{0,1:T(8,128)(2,1)}, u32[]{:S(2)}) copy-start(bf16[1024,384]{0,1:T(8,128)(2,1)} %copy-done.57) | copy-start | bytes 2359300
  162.1 16.4 %slice-start = ((s8[12582912]{0:T(1024)(128)(4,1)}), s8[4194304]{0:T(1024)(128)(4,1)S(1)}, s32[]{:S(2)}) async-start(s8[12582912]{0:T(1024)(128)(4,1)} %bitcast.224), calls=%async_computation.4 | async-start | bytes 8388608
  162.1 16.4 %slice-start.1 = ((s8[12582912]{0:T(1024)(128)(4,1)}), s8[4194304]{0:T(1024)(128)(4,1)S(1)}, s32[]{:S(2)}) async-start(s8[12582912]{0:T(1024)(128)(4,1)} %bitcast.224), calls=%async_computation.5 | async-start | bytes 8388608
  168.7 9.8 %slice-start.2 = ((s8[12582912]{0:T(1024)(128)(4,1)}), s8[4194304]{0:T(1024)(128)(4,1)S(1)}, s32[]{:S(2)}) async-start(s8[12582912]{0:T(1024)(128)(4,1)} %bitcast.224), calls=%async_computation.6 | async-start | bytes 8388608
  185.6 18.5 %copy-start.27 = (bf16[1024,384]{0,1:T(8,128)(2,1)S(1)}, bf16[1024,384]{0,1:T(8,128)(2,1)}, u32[]{:S(2)}) copy-start(bf16[1024,384]{0,1:T(8,128)(2,1)} %copy-done.26) | copy-start | bytes 2359300
  204.2 10.4 %slice-start.11 = ((s8[6291456]{0:T(1024)(128)(4,1)}), s8[4194304]{0:T(1024)(128)(4,1)S(1)}, s32[]{:S(2)}) async-start(s8[6291456]{0:T(1024)(128)(4,1)} %bitcast.234), calls=%async_computation.15 | async-start | bytes 8388608
  225.0 7.6 %collective-permute-start.7 = (bf16[512,768]{0,1:T(8,128)(2,1)S(1)}, bf16[512,768]{0,1:T(8,128)(2,1)S(1)}, u32[]{:S(2)}, u32[]{:S(2)}) collective-permute-start(bf16[512,768]{0,1:T(8,128)(2,1)S(1)} %broadcast_select_fusion.4), channel_id=1, source_target_pairs={{0,1},{1,0},{2,3},{3,2},{4,5},{5,4},{6,7},{7,6},{8,9},{9,8},{10,11... | collective-permute-start | bytes 2359304 | tf_op jit(solution)/shard_map/ppermute | solution.py:158
  234.5 5.0 %collective-permute-start.8 = (bf16[512,768]{0,1:T(8,128)(2,1)S(1)}, bf16[512,768]{0,1:T(8,128)(2,1)S(1)}, u32[]{:S(2)}, u32[]{:S(2)}) collective-permute-start(bf16[512,768]{0,1:T(8,128)(2,1)S(1)} %add_convert_fusion.9), channel_id=1, source_target_pairs={{0,1},{1,0},{2,3},{3,2},{4,5},{5,4},{6,7},{7,6},{8,9},{9,8},{10,11... | collective-permute-start | bytes 2359304 | tf_op jit(solution)/shard_map/ppermute | solution.py:158
  239.3 65.3 %collective-permute-start.11 = (f32[3072]{0:T(1024)}, f32[3072]{0:T(1024)}, u32[]{:S(2)}, u32[]{:S(2)}) collective-permute-start(f32[3072]{0:T(1024)} %pad_maximum_fusion.16), channel_id=1, source_target_pairs={{0,1},{1,0},{2,3},{3,2},{4,5},{5,4},{6,7},{7,6},{8,9},{9,8},{10,11... | collective-permute-start | bytes 36872 | tf_op jit(solution)/shard_map/ppermute | solution.py:158
  248.8 7.9 %copy-start.48 = (pred[256,512]{1,0:T(8,128)(4,1)S(1)}, pred[256,512]{1,0:T(8,128)(4,1)}, u32[]{:S(2)}) copy-start(pred[256,512]{1,0:T(8,128)(4,1)} %copy-done.47) | copy-start | bytes 393220
  248.8 7.9 %copy-start.66 = (bf16[1024,384]{0,1:T(8,128)(2,1)S(1)}, bf16[1024,384]{0,1:T(8,128)(2,1)}, u32[]{:S(2)}) copy-start(bf16[1024,384]{0,1:T(8,128)(2,1)} %copy-done.65) | copy-start | bytes 2359300
  248.8 7.9 %copy-start.93 = (bf16[512,384]{0,1:T(8,128)(2,1)S(1)}, bf16[512,384]{0,1:T(8,128)(2,1)}, u32[]{:S(2)}) copy-start(bf16[512,384]{0,1:T(8,128)(2,1)} %slice.599) | copy-start | bytes 1179652
  248.8 15.2 %slice-start.7 = ((s8[4718592]{0:T(1024)(128)(4,1)}), s8[524288]{0:T(1024)(128)(4,1)S(1)}, s32[]{:S(2)}) async-start(s8[4718592]{0:T(1024)(128)(4,1)} %bitcast.230), calls=%async_computation.11 | async-start | bytes 1048576
  248.8 84.3 %all-to-all-start.1 = ((bf16[16,48,1536]{2,1,0:T(8,128)(2,1)}), bf16[16,48,1536]{2,1,0:T(8,128)(2,1)}, u32[]{:S(2)}, u32[]{:S(2)}) async-start(bf16[16,48,1536]{2,1,0:T(8,128)(2,1)} %bitcast.71), calls=%async_computation.1 | async-start | bytes 4718592 | tf_op jit(solution)/shard_map/all_to_all | solution.py:323
  256.7 6.4 %copy-start.7 = (f32[6,256,512]{2,1,0:T(8,128)S(1)}, f32[6,256,512]{2,1,0:T(8,128)}, u32[]{:S(2)}) copy-start(f32[6,256,512]{2,1,0:T(8,128)} %copy-done.6) | copy-start | bytes 9437188
  256.8 7.3 %slice-start.8 = ((s8[4718592]{0:T(1024)(128)(4,1)}), s8[4194304]{0:T(1024)(128)(4,1)S(1)}, s32[]{:S(2)}) async-start(s8[4718592]{0:T(1024)(128)(4,1)} %bitcast.230), calls=%async_computation.12 | async-start | bytes 8388608
  263.1 6.0 %slice-start.3 = ((s8[6291456]{0:T(1024)(128)(4,1)}), s8[4194304]{0:T(1024)(128)(4,1)S(1)}, s32[]{:S(2)}) async-start(s8[6291456]{0:T(1024)(128)(4,1)} %bitcast.226), calls=%async_computation.7 | async-start | bytes 8388608
  273.2 6.5 %copy-start.56 = (bf16[512,384]{0,1:T(8,128)(2,1)S(1)}, bf16[512,384]{0,1:T(8,128)(2,1)}, u32[]{:S(2)}) copy-start(bf16[512,384]{0,1:T(8,128)(2,1)} %copy-done.55) | copy-start | bytes 1179652
  276.3 9.1 %slice-start.13 = ((s8[6291456]{0:T(1024)(128)(4,1)}), s8[4194304]{0:T(1024)(128)(4,1)S(1)}, s32[]{:S(2)}) async-start(s8[6291456]{0:T(1024)(128)(4,1)} %bitcast.236), calls=%async_computation.17 | async-start | bytes 8388608
  280.3 9.5 %copy-start.82 = (bf16[6,64,256]{2,1,0:T(8,128)(2,1)}, bf16[6,64,256]{2,1,0:T(8,128)(2,1)S(1)}, u32[]{:S(2)}) copy-start(bf16[6,64,256]{2,1,0:T(8,128)(2,1)S(1)} %convolution_convert_fusion.21) | copy-start | bytes 589828
  280.9 5.9 %slice-start.14 = ((s8[6291456]{0:T(1024)(128)(4,1)}), s8[2097152]{0:T(1024)(128)(4,1)S(1)}, s32[]{:S(2)}) async-start(s8[6291456]{0:T(1024)(128)(4,1)} %bitcast.236), calls=%async_computation.18 | async-start | bytes 4194304
  288.7 10.1 %copy-start.15 = (bf16[6,256,1024]{2,1,0:T(8,128)(2,1)}, bf16[6,256,1024]{2,1,0:T(8,128)(2,1)S(1)}, u32[]{:S(2)}) copy-start(bf16[6,256,1024]{2,1,0:T(8,128)(2,1)S(1)} %multiply_convert_fusion.2) | copy-start | bytes 9437188
  288.7 7.2 %copy-start.148 = (f32[384]{0:T(512)S(1)}, f32[384]{0:T(512)}, u32[]{:S(2)}) copy-start(f32[384]{0:T(512)} %reduce_sum.442) | copy-start | bytes 4612
  288.7 8.5 %copy-start.60 = (bf16[1024,6,64]{0,2,1:T(8,128)(2,1)S(1)}, bf16[1024,6,64]{0,2,1:T(8,128)(2,1)}, u32[]{:S(2)}) copy-start(bf16[1024,6,64]{0,2,1:T(8,128)(2,1)} %get-tuple-element.380) | copy-start | bytes 2359300
  288.8 8.5 %copy-start.118 = (bf16[1024,768]{1,0:T(8,128)(2,1)S(1)}, bf16[1024,768]{1,0:T(8,128)(2,1)}, u32[]{:S(2)}) copy-start(bf16[1024,768]{1,0:T(8,128)(2,1)} %param.64) | copy-start | bytes 4718596
  289.8 9.0 %copy-start.144 = (f32[768]{0:T(1024)S(1)}, f32[768]{0:T(1024)}, u32[]{:S(2)}) copy-start(f32[768]{0:T(1024)} %convert_reduce_fusion.5) | copy-start | bytes 9220
  300.1 16.8 %copy-start.79 = (bf16[256,384]{0,1:T(8,128)(2,1)S(1)}, bf16[256,384]{0,1:T(8,128)(2,1)}, u32[]{:S(2)}) copy-start(bf16[256,384]{0,1:T(8,128)(2,1)} %get-tuple-element.321) | copy-start | bytes 589828
  333.1 7.4 %copy-start.54 = (bf16[6,64,1024]{2,1,0:T(8,128)(2,1)S(1)}, bf16[6,64,1024]{2,1,0:T(8,128)(2,1)}, u32[]{:S(2)}) copy-start(bf16[6,64,1024]{2,1,0:T(8,128)(2,1)} %copy-done.53) | copy-start | bytes 2359300
  333.1 7.4 %copy-start.110 = (bf16[768,384]{1,0:T(8,128)(2,1)S(1)}, bf16[768,384]{1,0:T(8,128)(2,1)}, u32[]{:S(2)}) copy-start(bf16[768,384]{1,0:T(8,128)(2,1)} %param.77) | copy-start | bytes 1769476
  333.1 77.2 %all-to-all-start = ((bf16[16,62,1536]{2,1,0:T(8,128)(2,1)}), bf16[16,62,1536]{2,1,0:T(8,128)(2,1)}, u32[]{:S(2)}, u32[]{:S(2)}) async-start(bf16[16,62,1536]{2,1,0:T(8,128)(2,1)} %pad_maximum_fusion.1), calls=%async_computation | async-start | bytes 6291456 | tf_op jit(solution)/shard_map/all_to_all | solution.py:323
  343.9 7.1 %collective-permute-start.10 = (bf16[512,768]{0,1:T(8,128)(2,1)}, bf16[512,768]{0,1:T(8,128)(2,1)}, u32[]{:S(2)}, u32[]{:S(2)}) collective-permute-start(bf16[512,768]{0,1:T(8,128)(2,1)} %broadcast_select_fusion), channel_id=1, source_target_pairs={{0,1},{1,0},{2,3},{3,2},{4,5},{5,4},{6,7},{7,6},{8,9},{9,8},{10,11... | collective-permute-start | bytes 2359304 | tf_op jit(solution)/shard_map/ppermute | solution.py:158
  347.4 9.8 %collective-permute-start.9 = (bf16[512,768]{0,1:T(8,128)(2,1)S(1)}, bf16[512,768]{0,1:T(8,128)(2,1)S(1)}, u32[]{:S(2)}, u32[]{:S(2)}) collective-permute-start(bf16[512,768]{0,1:T(8,128)(2,1)S(1)} %broadcast_select_fusion.1), channel_id=1, source_target_pairs={{0,1},{1,0},{2,3},{3,2},{4,5},{5,4},{6,7},{7,6},{8,9},{9,8},{10,11... | collective-permute-start | bytes 2359304 | tf_op jit(solution)/shard_map/ppermute | solution.py:158
  351.0 6.2 %copy-start.19 = (f32[512,768]{0,1:T(8,128)S(1)}, f32[512,768]{0,1:T(8,128)}, u32[]{:S(2)}) copy-start(f32[512,768]{0,1:T(8,128)} %copy-done.18) | copy-start | bytes 4718596
  351.0 6.2 %copy-start.141 = (f32[512]{0:T(512)S(1)}, f32[512]{0:T(512)}, u32[]{:S(2)}) copy-start(f32[512]{0:T(512)} %copy-done.140) | copy-start | bytes 6148
  365.2 53.5 %copy-start.1 = (bf16[768,1536]{1,0:T(8,128)(2,1)S(1)}, bf16[768,1536]{1,0:T(8,128)(2,1)}, u32[]{:S(2)}) copy-start(bf16[768,1536]{1,0:T(8,128)(2,1)} %param.88) | copy-start | bytes 7077892
  (145 other events, 373.7 us)
Sparse Core Ops, SparseCore 0:
  156.9 165.7 reduce-scatter.1
where the time goes:
time: 433 us; the launch traced here: 426 us
  matrix products  168 us (39%)
  other arithmetic  94 us (22%)
  local copies, waits for them, and re-layouts  78.8 us (18%)
  waiting for transfers between devices  49.9 us (12%)
  starting transfers between devices  18.1 us (4%)
  between operations  17 us (4%)
    dot_general x30, matrix products, project(): return jnp.dot(data, weight, preferred_element_type=jnp.float32)  68 us
    all_to_all x2, waiting for transfers between devices, exchange_sum(): received = lax.all_to_all(blocks, 'dp', 0, 0, tiled=True)  44.4 us
    unnamed x402, local copies, waits for them, and re-layouts  40.8 us
    dot_general x6, matrix products, attend_backward(): jnp.einsum('qhe,khe->hqk', grad_piece, values[:end], preferred_element_ty...  30.1 us
    convert_element_type x5, other arithmetic, attend_backward(): grad_scores = (probs * (grad_probs - row_inner)).astype(jnp.bfloat16)  27.9 us
    dot_general x6, matrix products, attend_backward(): jnp.einsum('hqk,qhe->khe', grad_scores, piece, preferred_element_type=jnp...  18.9 us
    dot_general x6, matrix products, attend_backward(): jnp.einsum('hqk,qhe->khe', probs.astype(jnp.bfloat16), grad_piece, prefer...  17.3 us
    all_to_all x2, starting transfers between devices, exchange_sum(): received = lax.all_to_all(blocks, 'dp', 0, 0, tiled=True)  15.3 us
  transfers between devices with their start and end apart: 15, of which 4 were waited for; matrix products, arithmetic and copies ran while one was open for 50% of the time, Pallas kernels for 0%

commit v1 on v0

--- a/solution.py
+++ b/solution.py
@@ -275,10 +275,61 @@
     grad_self_output_bias = column_sums(grad_self)
     grad_self_context = heads_of(project(grad_self, self_output.T).astype(jnp.bfloat16))
     dp_size = lax.axis_size("dp")
+
+    def pack(joined, vector):
+        width = joined.shape[1]
+        lines = -(-vector.shape[0] // width)
+        padded = jnp.pad(vector, (0, lines * width - vector.shape[0])).reshape(lines, width)
+        high = padded.astype(jnp.bfloat16)
+        low = (padded - high.astype(jnp.float32)).astype(jnp.bfloat16)
+        extra = jnp.concatenate([high, low], 0)
+        blocks = joined.reshape(dp_size, joined.shape[0] // dp_size, width)
+        return jnp.concatenate(
+            [blocks, jnp.broadcast_to(extra[None], (dp_size,) + extra.shape)], 1
+        )
+
+    def exchange(blocks, rows, pieces, flipped, count):
+        total = jnp.sum(lax.all_to_all(blocks, "dp", 0, 0, tiled=True).astype(jnp.float32), 0)
+        lines = (total.shape[0] - rows) // 2
+        vector = (total[rows : rows + lines] + total[rows + lines :]).reshape(-1)[:count]
+        parts = []
+        offset = 0
+        for position, piece in enumerate(pieces):
+            width = piece.shape[1]
+            part = total[:rows, offset : offset + width]
+            offset += width
+            if position in flipped:
+                part = part.T
+            parts.append(part)
+        return parts, vector
+
     grad_cross_output_t = project(grad_cross.T, cross_context)
-    cross = [grad_cross_query, grad_cross_key, grad_cross_value, grad_cross_output_t]
-    cross_joined = jnp.concatenate(cross, 1).astype(jnp.bfloat16)
-    cross_joined, grad_self_context = lax.optimization_barrier((cross_joined, grad_self_context))
+    grad_self_output_t = project(grad_self.T, self_context)
+    norm_pairs = sum_pair(
+        jnp.concatenate([grad_first_gain, grad_first_shift, grad_second_gain, grad_second_shift])
+    )
+    early_vector = jnp.concatenate(
+        [
+            grad_self_output_bias,
+            grad_cross_query_bias,
+            grad_cross_value_bias,
+            grad_cross_output_bias,
+            norm_pairs,
+            grad_third_gain,
+            grad_third_shift,
+            grad_inner_bias,
+            grad_outer_bias,
+        ]
+    )
+    cross = [
+        grad_cross_query,
+        grad_cross_key,
+        grad_cross_value,
+        grad_cross_output_t,
+        grad_self_output_t,
+    ]
+    cross_blocks = pack(jnp.concatenate(cross, 1).astype(jnp.bfloat16), early_vector)
+    cross_blocks, grad_self_context = lax.optimization_barrier((cross_blocks, grad_self_context))
     self_grad_q, self_grad_k, self_grad_v = attend_backward(
         self_queries, self_keys, self_values, grad_self_context, self_totals, segment, True
     )
@@ -298,68 +349,29 @@
     tokens_part = scatter_rows(tokens_term.astype(jnp.bfloat16))
     memory_part = scatter_rows(memory_term.astype(jnp.bfloat16))
     grad_tokens = tokens_part + grad_first_in
-    grad_self_output_t = project(grad_self.T, self_context)
     grad_outer_weight_t = project(grad_outer.T, hidden)
 
-    def split_columns(summed, pieces, flipped):
-        parts = []
-        offset = 0
-        for position, piece in enumerate(pieces):
-            width = piece.shape[1]
-            part = summed[:, offset : offset + width]
-            offset += width
-            if position in flipped:
-                part = part.T
-            parts.append(part)
-        return parts
-
-    def exchange_sum(joined, extra=None):
-        rows = joined.shape[0] // dp_size
-        blocks = joined.reshape(dp_size, rows, joined.shape[1])
-        if extra is not None:
-            blocks = jnp.concatenate(
-                [blocks, jnp.broadcast_to(extra[None], (dp_size,) + extra.shape)], 1
-            )
-        received = lax.all_to_all(blocks, "dp", 0, 0, tiled=True)
-        return jnp.sum(received.astype(jnp.float32), 0)
-
+    rows = grad_inner_weight.shape[0] // dp_size
     ffn = [grad_inner_weight, grad_outer_weight_t]
     ffn_sum = lax.psum_scatter(
         jnp.concatenate(ffn, 1).astype(jnp.bfloat16), "dp", scatter_dimension=0, tiled=True
     ).astype(jnp.float32)
-    ffn_sums = split_columns(ffn_sum, ffn, (1,))
-    cross_sums = split_columns(exchange_sum(cross_joined), cross, (3,))
-    late = [grad_self_query, grad_self_key, grad_self_value, grad_self_output_t]
-    late_joined = jnp.concatenate(late, 1).astype(jnp.bfloat16)
-    norm_pairs = sum_pair(
-        jnp.concatenate([grad_first_gain, grad_first_shift, grad_second_gain, grad_second_shift])
-    )
-    vector = jnp.concatenate(
-        [
-            grad_self_query_bias,
-            grad_self_value_bias,
-            grad_self_output_bias,
-            grad_cross_query_bias,
-            grad_cross_value_bias,
-            grad_cross_output_bias,
-            norm_pairs,
-            grad_third_gain,
-            grad_third_shift,
-            grad_inner_bias,
-            grad_outer_bias,
-        ]
-    )
-    width = late_joined.shape[1]
-    lines = -(-vector.shape[0] // width)
-    padded = jnp.pad(vector, (0, lines * width - vector.shape[0])).reshape(lines, width)
-    high = padded.astype(jnp.bfloat16)
-    low = (padded - high.astype(jnp.float32)).astype(jnp.bfloat16)
-    late_rows = late_joined.shape[0] // dp_size
-    late_total = exchange_sum(late_joined, jnp.concatenate([high, low], 0))
-    self_sums = split_columns(late_total[:late_rows], late, (3,))
-    total = (
-        late_total[late_rows : late_rows + lines] + late_total[late_rows + lines :]
-    ).reshape(-1)
+    ffn_sums = [ffn_sum[:, : ffn[0].shape[1]], ffn_sum[:, ffn[0].shape[1] :].T]
+    cross_parts, early_total = exchange(
+        cross_blocks, rows, cross, (3, 4), early_vector.shape[0]
+    )
+    cross_sums = cross_parts[0:4]
+    late = [grad_self_query, grad_self_key, grad_self_value]
+    late_vector = jnp.concatenate([grad_self_query_bias, grad_self_value_bias])
+    self_sums, late_total = exchange(
+        pack(jnp.concatenate(late, 1).astype(jnp.bfloat16), late_vector),
+        rows,
+        late,
+        (),
+        late_vector.shape[0],
+    )
+    self_sums.append(cross_parts[4])
+    total = jnp.concatenate([late_total, early_total])
     smalls = []
     offset = 0
     for piece in (

time: 433 us -> 524 us (1.21)
  the two profiles are of different devices: /device:TPU:12 before, /device:TPU:0 now
where the time goes in v1:
time: 524 us; the launch traced here: 514 us
  matrix products  155 us (30%)
  waiting for transfers between devices  149 us (28%)
  other arithmetic  92.5 us (18%)
  local copies, waits for them, and re-layouts  69.5 us (13%)
  starting transfers between devices  30.8 us (6%)
  between operations  17.6 us (3%)
    reduce_scatter x1, waiting for transfers between devices, on_device(): lax.psum_scatter(jnp.concatenate(ffn, 1).astype(jnp.bfloat16), 'dp', scat...  92.5 us
    dot_general x30, matrix products, project(): return jnp.dot(data, weight, preferred_element_type=jnp.float32)  76.3 us
    all_to_all x2, waiting for transfers between devices, exchange(): lax.all_to_all(blocks, 'dp', 0, 0, tiled=True).astype(jnp.float32)  51.5 us
    unnamed x431, local copies, waits for them, and re-layouts  37 us
    all_to_all x2, starting transfers between devices, exchange(): lax.all_to_all(blocks, 'dp', 0, 0, tiled=True).astype(jnp.float32)  26.8 us
    dot_general x6, matrix products, attend_backward(): jnp.einsum('qhe,khe->hqk', grad_piece, values[:end], preferred_element_ty...  22.9 us
    convert_element_type x5, other arithmetic, attend_backward(): grad_scores = (probs * (grad_probs - row_inner)).astype(jnp.bfloat16)  22.1 us
    dot_general x6, matrix products, attend_backward(): jnp.einsum('hqk,qhe->khe', probs.astype(jnp.bfloat16), grad_piece, prefer...  15.2 us
  transfers between devices with their start and end apart: 15, of which 5 were waited for; matrix products, arithmetic and copies ran while one was open for 15% of the time, Pallas kernels for 0%

profile of v1, /device:TPU:0, one launch (start us, length us, event | category | flops | bytes accessed | tf_op | source)
XLA Modules:
  0.0 513.8 jit_solution(731334597434745419)
XLA Ops:
  10.6 2.4 convolution_convert_fusion.9
  22.1 1.7 select_reduce_fusion.4
  29.0 1.7 fusion.90
  34.9 2.3 fusion.92
  39.6 2.7 fusion.165
  42.3 3.4 slice_select_fusion
  49.6 2.9 fusion.155
  58.0 2.1 select_reduce_fusion.1
  60.2 3.4 fusion
  64.8 4.5 fusion.88
  69.3 2.1 select_reduce_fusion
  71.5 3.4 fusion.1
  76.0 4.1 fusion.87
  81.9 1.9 collective-permute-done.2
  85.5 1.9 collective-permute-done.3
  88.0 18.2 %multiply_convert_fusion.3 = (bf16[1024,1536]{1,0:T(8,128)(2,1)S(1)}, f32[1024,1536]{1,0:T(8,128)}, f32[1024,1536]{1,0:T(8,128)}) fusion(f32[1536]{0:T(1024)S(1)} %convert_element_type.352, bf16[768,1536]{1,0:T(8,128)(2,1)S(1)} %copy-done, bf16[512,768]{0,1:T(8,128)(2,1)S(1)} %get-tuple-element.314, bf16[512,768]{0,1:T(8,128)(2,1)S(1)} %get-tuple-element.313), kind=kOutput, calls=%fused_computation.28 | convolution fusion | flops 2522873856 | bytes 19666944 | tf_op jit(solution)/shard_map/dot_general | solution.py:22
  106.2 3.8 convolution_convert_fusion.5
  111.0 2.7 copy.85
  113.9 3.2 fusion.152
  117.1 1.6 fusion.27
  118.8 2.2 fusion.30
  120.9 3.3 convert_reduce_fusion.4
  124.2 8.6 %convert_reduce_fusion.1 = (f32[1536]{0:T(1024)}, bf16[1024,1536]{1,0:T(8,128)(2,1)S(1)}) fusion(f32[1024,1536]{1,0:T(8,128)S(1)} %bitcast.340, bf16[1536,768]{1,0:T(8,128)(2,1)S(1)} %copy-done.186, f32[1024,768]{0,1:T(8,128)S(1)} %get-tuple-element.293, f32[1024,1536]{1,0:T(8,128)} %get-tuple-element.366, f32[1536]{0:T(1024)S(1)} %copy-done.167), kind=kOutput, calls=%fused_computation.24 | convolution fusion | flops 2443442688 | bytes 21245952 | tf_op jit(solution)/shard_map/dot_general | solution.py:22
  132.8 2.6 convolution_convert_fusion.4
  138.6 1.7 copy.93
  140.3 1.7 copy.94
  142.0 1.7 copy.95
  143.8 1.8 copy.92
  148.1 3.7 multiply_reduce_fusion.7
  154.7 3.8 convolution_convert_fusion.1
  158.5 4.1 convolution_convert_fusion
  165.8 7.2 %multiply_reduce_fusion.1 = (f32[6,512]{1,0:T(8,128)S(1)}, f32[6,512,1024]{2,1,0:T(8,128)}) fusion(f32[6,512,1024]{2,1,0:T(8,128)S(1)} %bitcast.235, f32[6,512]{1,0:T(8,128)S(1)} %log_add_fusion.1, pred[512,1024]{1,0:T(8,128)(4,1)S(1)} %get-tuple-element.346, bf16[512,6,64]{0,2,1:T(8,128)(2,1)S(1)} %bitcast.261, bf16[1024,6,64]{0,2,1:T(8,128)(2,1)S(1)} %bitcast.267), kind=kOutput, calls=%fused_computation.4 | convolution fusion | flops 415233024 | bytes 26894336 | tf_op jit(solution)/shard_map/qhe,khe->hqk/dot_general | solution.py:89
  173.0 9.6 %multiply_reduce_fusion = (f32[6,512]{1,0:T(8,128)S(1)}, f32[6,512,1024]{2,1,0:T(8,128)}) fusion(f32[6,512,1024]{2,1,0:T(8,128)} %copy-done.3, f32[6,512]{1,0:T(8,128)S(1)} %log_add_fusion, pred[512,1024]{1,0:T(8,128)(4,1)S(1)} %get-tuple-element.347, bf16[512,6,64]{0,2,1:T(8,128)(2,1)S(1)} %bitcast.263, bf16[1024,6,64]{0,2,1:T(8,128)(2,1)S(1)} %bitcast.268), kind=kOutput, calls=%fused_computation.1 | convolution fusion | flops 415233024 | bytes 26894336 | tf_op jit(solution)/shard_map/qhe,khe->hqk/dot_general | solution.py:89
  182.6 17.6 %multiply_convert_fusion = (bf16[6,512,1024]{2,1,0:T(8,128)(2,1)}, bf16[6,512,1024]{2,1,0:T(8,128)(2,1)}) fusion(f32[6,512,1024]{2,1,0:T(8,128)} %get-tuple-element.368, f32[6,512,1024]{2,1,0:T(8,128)} %copy-done.3, f32[6,512]{1,0:T(8,128)S(1)} %get-tuple-element.367, f32[6,512]{1,0:T(8,128)S(1)} %log_add_fusion, pred[512,1024]{1,0:T(8,128)(4,1)S(1)} %get-tuple-element.347, ...), kind=kLoop, calls=%fused_computation | loop fusion | flops 31457280 | bytes 64012288 | tf_op jit(solution)/shard_map/convert_element_type | solution.py:93
  200.2 5.7 %convolution_convert_fusion.19 = bf16[6,64,512]{2,1,0:T(8,128)(2,1)} fusion(bf16[1024,6,64]{0,2,1:T(8,128)(2,1)S(1)} %bitcast.244, bf16[6,512,1024]{2,1,0:T(8,128)(2,1)} %get-tuple-element.386), kind=kOutput, calls=%fused_computation.188 | convolution fusion | flops 402849792 | bytes 7471104 | tf_op jit(solution)/shard_map/hqk,khe->qhe/dot_general | solution.py:95
  207.1 6.8 %fusion.4 = f32[6,64,1024]{2,1,0:T(8,128)S(1)} fusion(bf16[512,6,64]{0,2,1:T(8,128)(2,1)S(1)} %bitcast.264, f32[6,512,1024]{2,1,0:T(8,128)} %copy-done.3, f32[6,512]{1,0:T(8,128)S(1)} %log_add_fusion, pred[512,1024]{1,0:T(8,128)(4,1)S(1)} %get-tuple-element.347), kind=kOutput, calls=%fused_computation.18 | convolution fusion | flops 412090368 | bytes 15085568 | tf_op jit(solution)/shard_map/hqk,qhe->khe/dot_general | solution.py:101
  214.0 2.0 convolution_convert_fusion.18
  219.7 4.0 convert_reduce_fusion.9
  225.6 3.1 fusion.83
  228.7 2.2 copy.88
  232.1 2.6 convolution_convert_fusion.17
  235.0 2.2 multiply_reduce_fusion.8
  244.3 3.2 fusion.68
  247.6 4.4 pad_maximum_fusion.1
  259.3 2.0 multiply_reduce_fusion.3
  265.2 2.3 multiply_reduce_fusion.2
  267.5 1.9 multiply_convert_fusion.2
  272.0 1.6 fusion.84
  276.7 1.8 convert_reduce_fusion.7
  281.1 3.0 fusion.86
  286.9 1.9 fusion.74
  294.9 8.1 %all-to-all-start = ((bf16[16,50,1152]{2,1,0:T(8,128)(2,1)}), bf16[16,50,1152]{2,1,0:T(8,128)(2,1)S(1)}, u32[]{:S(2)}, u32[]{:S(2)}) async-start(bf16[16,50,1152]{2,1,0:T(8,128)(2,1)} %pad_maximum_fusion.2), calls=%async_computation | async-start | bytes 4128768 | tf_op jit(solution)/shard_map/all_to_all | solution.py:292
  303.1 5.1 pad_maximum_fusion
  308.2 51.5 %all-to-all-done = bf16[16,50,1152]{2,1,0:T(8,128)(2,1)S(1)} async-done(((bf16[16,50,1152]{2,1,0:T(8,128)(2,1)}), bf16[16,50,1152]{2,1,0:T(8,128)(2,1)S(1)}, u32[]{:S(2)}, u32[]{:S(2)}) %all-to-all-start) | async-done | bytes 1843232 | tf_op jit(solution)/shard_map/all_to_all | solution.py:292
  361.0 18.7 %all-to-all-start.1 = ((bf16[16,58,1920]{2,1,0:T(8,128)(2,1)}), bf16[16,58,1920]{2,1,0:T(8,128)(2,1)}, u32[]{:S(2)}, u32[]{:S(2)}) async-start(bf16[16,58,1920]{2,1,0:T(8,128)(2,1)} %pad_maximum_fusion.1), calls=%async_computation.1 | async-start | bytes 7864320 | tf_op jit(solution)/shard_map/all_to_all | solution.py:292
  379.7 2.2 fusion.168
  388.4 2.6 copy.107
  390.9 3.2 convert_add_fusion
  394.2 3.0 copy.109
  397.2 3.2 add_add_fusion.4
  400.4 3.2 copy.108
  405.2 92.5 %reduce-scatter.2.cloned.1.call-done = bf16[48,3072]{1,0:T(8,128)(2,1)} async-done(((bf16[768,3072]{1,0:T(8,128)(2,1)}), bf16[48,3072]{1,0:T(8,128)(2,1)}) %reduce-scatter.2.cloned.1.call-update) | async-done | bytes 294928 | tf_op jit(solution)/shard_map/reduce_scatter | solution.py:356
  498.7 1.8 slice.672
  501.2 2.7 convert_reduce_fusion
  (614 shorter events, 108.0 us)
Async XLA Ops:
  7.2 80.8 %copy-start = (bf16[768,1536]{1,0:T(8,128)(2,1)S(1)}, bf16[768,1536]{1,0:T(8,128)(2,1)}, u32[]{:S(2)}) copy-start(bf16[768,1536]{1,0:T(8,128)(2,1)} %param.88) | copy-start | bytes 7077892
  7.2 6.8 %copy-start.125 = (bf16[1024,768]{1,0:T(8,128)(2,1)S(1)}, bf16[1024,768]{1,0:T(8,128)(2,1)}, u32[]{:S(2)}) copy-start(bf16[1024,768]{1,0:T(8,128)(2,1)} %param.64) | copy-start | bytes 4718596
  7.2 6.8 %copy-start.181 = (bf16[384]{0:T(512)(128)(2,1)S(1)}, bf16[384]{0:T(512)(128)(2,1)}, u32[]{:S(2)}) copy-start(bf16[384]{0:T(512)(128)(2,1)} %param.72) | copy-start | bytes 2308
  7.2 6.8 %copy-start.123 = (bf16[768,384]{1,0:T(8,128)(2,1)S(1)}, bf16[768,384]{1,0:T(8,128)(2,1)}, u32[]{:S(2)}) copy-start(bf16[768,384]{1,0:T(8,128)(2,1)} %param.71) | copy-start | bytes 1769476
  13.0 18.2 %copy-start.29 = (bf16[1024,384]{0,1:T(8,128)(2,1)}, bf16[1024,384]{0,1:T(8,128)(2,1)S(1)}, u32[]{:S(2)}) copy-start(bf16[1024,384]{0,1:T(8,128)(2,1)S(1)} %convolution_convert_fusion.9) | copy-start | bytes 2359300
  13.0 9.0 %copy-start.60 = (bf16[512,384]{0,1:T(8,128)(2,1)}, bf16[512,384]{0,1:T(8,128)(2,1)S(1)}, u32[]{:S(2)}) copy-start(bf16[512,384]{0,1:T(8,128)(2,1)S(1)} %slice.625) | copy-start | bytes 1179652
  26.1 12.8 %copy-start.113 = (bf16[6,64,256]{2,1,0:T(8,128)(2,1)}, bf16[6,64,256]{2,1,0:T(8,128)(2,1)S(1)}, u32[]{:S(2)}) copy-start(bf16[6,64,256]{2,1,0:T(8,128)(2,1)S(1)} %fusion.91) | copy-start | bytes 589828
  30.7 8.2 %copy-start.114 = (bf16[6,64,256]{2,1,0:T(8,128)(2,1)}, bf16[6,64,256]{2,1,0:T(8,128)(2,1)S(1)}, u32[]{:S(2)}) copy-start(bf16[6,64,256]{2,1,0:T(8,128)(2,1)S(1)} %fusion.90) | copy-start | bytes 589828
  42.2 6.3 %copy-start.170 = (bf16[768]{0:T(1024)(128)(2,1)S(1)}, bf16[768]{0:T(1024)(128)(2,1)}, u32[]{:S(2)}) copy-start(bf16[768]{0:T(1024)(128)(2,1)} %param.74) | copy-start | bytes 4612
  42.2 6.3 %copy-start.171 = (bf16[768]{0:T(1024)(128)(2,1)S(1)}, bf16[768]{0:T(1024)(128)(2,1)}, u32[]{:S(2)}) copy-start(bf16[768]{0:T(1024)(128)(2,1)} %param.82) | copy-start | bytes 4612
  42.2 6.3 %copy-start.172 = (bf16[768]{0:T(1024)(128)(2,1)S(1)}, bf16[768]{0:T(1024)(128)(2,1)}, u32[]{:S(2)}) copy-start(bf16[768]{0:T(1024)(128)(2,1)} %param.83) | copy-start | bytes 4612
  42.2 6.3 %copy-start.183 = (bf16[384]{0:T(512)(128)(2,1)S(1)}, bf16[384]{0:T(512)(128)(2,1)}, u32[]{:S(2)}) copy-start(bf16[384]{0:T(512)(128)(2,1)} %param.76) | copy-start | bytes 2308
  42.3 6.3 %copy-start.184 = (bf16[384]{0:T(512)(128)(2,1)S(1)}, bf16[384]{0:T(512)(128)(2,1)}, u32[]{:S(2)}) copy-start(bf16[384]{0:T(512)(128)(2,1)} %param.79) | copy-start | bytes 2308
  45.7 3.9 collective-permute-start
  48.6 35.3 %copy-start.135 = (f32[768]{0:T(1024)}, f32[768]{0:T(1024)S(1)}, u32[]{:S(2)}) copy-start(f32[768]{0:T(1024)S(1)} %convert_element_type.333) | copy-start | bytes 9220
  52.5 31.3 %copy-start.8 = (f32[512,768]{0,1:T(8,128)}, f32[512,768]{0,1:T(8,128)S(1)}, u32[]{:S(2)}) copy-start(f32[512,768]{0,1:T(8,128)S(1)} %get-tuple-element.307) | copy-start | bytes 4718596
  52.5 31.3 %copy-start.140 = (f32[512]{0:T(512)}, f32[512]{0:T(512)S(1)}, u32[]{:S(2)}) copy-start(f32[512]{0:T(512)S(1)} %broadcast_multiply_fusion.2) | copy-start | bytes 6148
  52.8 31.0 %copy-start.142 = (f32[512]{0:T(512)}, f32[512]{0:T(512)S(1)}, u32[]{:S(2)}) copy-start(f32[512]{0:T(512)S(1)} %fusion.123) | copy-start | bytes 6148
  53.1 3.3 collective-permute-start.1
  55.5 13.8 %copy-start.27 = (bf16[1024,384]{0,1:T(8,128)(2,1)}, bf16[1024,384]{0,1:T(8,128)(2,1)S(1)}, u32[]{:S(2)}) copy-start(bf16[1024,384]{0,1:T(8,128)(2,1)S(1)} %convolution_convert_fusion.8) | copy-start | bytes 2359300
  56.4 18.5 %copy-start.64 = (bf16[1024,384]{0,1:T(8,128)(2,1)}, bf16[1024,384]{0,1:T(8,128)(2,1)S(1)}, u32[]{:S(2)}) copy-start(bf16[1024,384]{0,1:T(8,128)(2,1)S(1)} %add_convert_fusion.7) | copy-start | bytes 2359300
  58.0 11.3 %copy-start.53 = (bf16[512,384]{0,1:T(8,128)(2,1)}, bf16[512,384]{0,1:T(8,128)(2,1)S(1)}, u32[]{:S(2)}) copy-start(bf16[512,384]{0,1:T(8,128)(2,1)S(1)} %get-tuple-element.320) | copy-start | bytes 1179652
  69.3 10.9 %copy-start.101 = (bf16[6,64,512]{2,1,0:T(8,128)(2,1)}, bf16[6,64,512]{2,1,0:T(8,128)(2,1)S(1)}, u32[]{:S(2)}) copy-start(bf16[6,64,512]{2,1,0:T(8,128)(2,1)S(1)} %fusion.88) | copy-start | bytes 1179652
  81.5 2.4 collective-permute-start.2
  85.1 2.4 collective-permute-start.3
  85.5 20.7 %copy-start.166 = (f32[1536]{0:T(1024)}, f32[1536]{0:T(1024)S(1)}, u32[]{:S(2)}) copy-start(f32[1536]{0:T(1024)S(1)} %convert_element_type.352) | copy-start | bytes 18436
  87.9 18.2 %copy-start.68 = (bf16[512,768]{0,1:T(8,128)(2,1)}, bf16[512,768]{0,1:T(8,128)(2,1)S(1)}, u32[]{:S(2)}) copy-start(bf16[512,768]{0,1:T(8,128)(2,1)S(1)} %get-tuple-element.313) | copy-start | bytes 2359300
  88.0 18.2 %copy-start.70 = (bf16[512,768]{0,1:T(8,128)(2,1)}, bf16[512,768]{0,1:T(8,128)(2,1)S(1)}, u32[]{:S(2)}) copy-start(bf16[512,768]{0,1:T(8,128)(2,1)S(1)} %get-tuple-element.314) | copy-start | bytes 2359300
  88.0 18.2 %copy-start.185 = (bf16[1536,768]{1,0:T(8,128)(2,1)S(1)}, bf16[1536,768]{1,0:T(8,128)(2,1)}, u32[]{:S(2)}) copy-start(bf16[1536,768]{1,0:T(8,128)(2,1)} %param.90) | copy-start | bytes 7077892
  110.0 3.9 collective-permute-start.4
  117.1 7.1 %slice-start.9 = ((s8[6291456]{0:T(1024)(128)(4,1)}), s8[4194304]{0:T(1024)(128)(4,1)S(1)}, s32[]{:S(2)}) async-start(s8[6291456]{0:T(1024)(128)(4,1)} %bitcast.339), calls=%async_computation.13 | async-start | bytes 8388608
  124.2 8.6 %copy-start.35 = (f32[1024,768]{0,1:T(8,128)}, f32[1024,768]{0,1:T(8,128)S(1)}, u32[]{:S(2)}) copy-start(f32[1024,768]{0,1:T(8,128)S(1)} %get-tuple-element.293) | copy-start | bytes 9437188
  136.6 9.5 %copy-start.102 = (bf16[6,64,512]{2,1,0:T(8,128)(2,1)S(1)}, bf16[6,64,512]{2,1,0:T(8,128)(2,1)}, u32[]{:S(2)}) copy-start(bf16[6,64,512]{2,1,0:T(8,128)(2,1)} %copy-done.101) | copy-start | bytes 1179652
  136.6 10.4 %copy-start.104 = (bf16[6,64,512]{2,1,0:T(8,128)(2,1)S(1)}, bf16[6,64,512]{2,1,0:T(8,128)(2,1)}, u32[]{:S(2)}) copy-start(bf16[6,64,512]{2,1,0:T(8,128)(2,1)} %copy-done.103) | copy-start | bytes 1179652
  136.6 11.4 %copy-start.12 = (f32[512,768]{0,1:T(8,128)S(1)}, f32[512,768]{0,1:T(8,128)}, u32[]{:S(2)}) copy-start(f32[512,768]{0,1:T(8,128)} %copy-done.11) | copy-start | bytes 4718596
  137.6 10.4 %collective-permute-start.5 = (bf16[512,768]{0,1:T(8,128)(2,1)}, bf16[512,768]{0,1:T(8,128)(2,1)}, u32[]{:S(2)}, u32[]{:S(2)}) collective-permute-start(bf16[512,768]{0,1:T(8,128)(2,1)} %broadcast_select_fusion.7), channel_id=1, source_target_pairs={{0,1},{1,0},{2,3},{3,2},{4,5},{5,4},{6,7},{7,6},{8,9},{9,8},{10,11... | collective-permute-start | bytes 2359304 | tf_op jit(solution)/shard_map/ppermute | solution.py:158
  152.2 10.4 %copy-start.20 = (f32[512,768]{0,1:T(8,128)}, f32[512,768]{0,1:T(8,128)S(1)}, u32[]{:S(2)}) copy-start(f32[512,768]{0,1:T(8,128)S(1)} %get-tuple-element.298) | copy-start | bytes 4718596
  152.2 10.4 %copy-start.155 = (f32[512]{0:T(512)}, f32[512]{0:T(512)S(1)}, u32[]{:S(2)}) copy-start(f32[512]{0:T(512)S(1)} %negate_multiply_fusion.3) | copy-start | bytes 6148
  152.5 6.1 %copy-start.36 = (f32[1024,768]{0,1:T(8,128)S(1)}, f32[1024,768]{0,1:T(8,128)}, u32[]{:S(2)}) copy-start(f32[1024,768]{0,1:T(8,128)} %copy-done.35) | copy-start | bytes 9437188
  152.5 6.1 %copy-start.194 = (bf16[1024,1536]{1,0:T(8,128)(2,1)S(1)}, bf16[1024,1536]{1,0:T(8,128)(2,1)}, u32[]{:S(2)}) copy-start(bf16[1024,1536]{1,0:T(8,128)(2,1)} %copy-done.193) | copy-start | bytes 9437188
  152.5 10.2 %collective-permute-start.6 = (bf16[512,768]{0,1:T(8,128)(2,1)S(1)}, bf16[512,768]{0,1:T(8,128)(2,1)S(1)}, u32[]{:S(2)}, u32[]{:S(2)}) collective-permute-start(bf16[512,768]{0,1:T(8,128)(2,1)S(1)} %add_convert_fusion.10), channel_id=1, source_target_pairs={{0,1},{1,0},{2,3},{3,2},{4,5},{5,4},{6,7},{7,6},{8,9},{9,8},{10,11... | collective-permute-start | bytes 2359304 | tf_op jit(solution)/shard_map/ppermute | solution.py:158
  164.1 8.9 %copy-start.62 = (bf16[512,384]{0,1:T(8,128)(2,1)}, bf16[512,384]{0,1:T(8,128)(2,1)S(1)}, u32[]{:S(2)}) copy-start(bf16[512,384]{0,1:T(8,128)(2,1)S(1)} %get-tuple-element.317) | copy-start | bytes 1179652
  182.6 17.6 %copy-start.28 = (bf16[1024,384]{0,1:T(8,128)(2,1)S(1)}, bf16[1024,384]{0,1:T(8,128)(2,1)}, u32[]{:S(2)}) copy-start(bf16[1024,384]{0,1:T(8,128)(2,1)} %copy-done.27) | copy-start | bytes 2359300
  205.9 8.0 %slice-start.7 = ((s8[6291456]{0:T(1024)(128)(4,1)}), s8[4194304]{0:T(1024)(128)(4,1)S(1)}, s32[]{:S(2)}) async-start(s8[6291456]{0:T(1024)(128)(4,1)} %bitcast.240), calls=%async_computation.11 | async-start | bytes 8388608
  207.1 6.8 %slice-start.8 = ((s8[6291456]{0:T(1024)(128)(4,1)}), s8[2097152]{0:T(1024)(128)(4,1)S(1)}, s32[]{:S(2)}) async-start(s8[6291456]{0:T(1024)(128)(4,1)} %bitcast.240), calls=%async_computation.12 | async-start | bytes 4194304
  218.1 16.7 %collective-permute-start.7 = (bf16[512,768]{0,1:T(8,128)(2,1)}, bf16[512,768]{0,1:T(8,128)(2,1)}, u32[]{:S(2)}, u32[]{:S(2)}) collective-permute-start(bf16[512,768]{0,1:T(8,128)(2,1)} %broadcast_select_fusion.4), channel_id=1, source_target_pairs={{0,1},{1,0},{2,3},{3,2},{4,5},{5,4},{6,7},{7,6},{8,9},{9,8},{10,11... | collective-permute-start | bytes 2359304 | tf_op jit(solution)/shard_map/ppermute | solution.py:158
  225.5 6.0 %copy-start.100 = (bf16[6,64,512]{2,1,0:T(8,128)(2,1)S(1)}, bf16[6,64,512]{2,1,0:T(8,128)(2,1)}, u32[]{:S(2)}) copy-start(bf16[6,64,512]{2,1,0:T(8,128)(2,1)} %copy-done.99) | copy-start | bytes 1179652
  225.5 6.2 %copy-start.40 = (bf16[512,768]{0,1:T(8,128)(2,1)S(1)}, bf16[512,768]{0,1:T(8,128)(2,1)}, u32[]{:S(2)}) copy-start(bf16[512,768]{0,1:T(8,128)(2,1)} %copy-done.39) | copy-start | bytes 2359300
  225.6 6.2 %copy-start.42 = (bf16[512,768]{0,1:T(8,128)(2,1)S(1)}, bf16[512,768]{0,1:T(8,128)(2,1)}, u32[]{:S(2)}) copy-start(bf16[512,768]{0,1:T(8,128)(2,1)} %copy-done.41) | copy-start | bytes 2359300
  238.0 3.1 collective-permute-start.8
  240.8 3.2 collective-permute-start.9
  242.1 11.1 %copy-start.74 = (bf16[1024,384]{0,1:T(8,128)(2,1)}, bf16[1024,384]{0,1:T(8,128)(2,1)S(1)}, u32[]{:S(2)}) copy-start(bf16[1024,384]{0,1:T(8,128)(2,1)S(1)} %convolution_convert_fusion.6) | copy-start | bytes 2359300
  254.5 19.1 %copy-start.86 = (bf16[6,64,256]{2,1,0:T(8,128)(2,1)}, bf16[6,64,256]{2,1,0:T(8,128)(2,1)S(1)}, u32[]{:S(2)}) copy-start(bf16[6,64,256]{2,1,0:T(8,128)(2,1)S(1)} %convolution_convert_fusion.23) | copy-start | bytes 589828
  259.3 14.3 %copy-start.88 = (bf16[6,64,256]{2,1,0:T(8,128)(2,1)}, bf16[6,64,256]{2,1,0:T(8,128)(2,1)S(1)}, u32[]{:S(2)}) copy-start(bf16[6,64,256]{2,1,0:T(8,128)(2,1)S(1)} %convolution_convert_fusion.21) | copy-start | bytes 589828
  265.2 8.4 %copy-start.90 = (bf16[6,64,256]{2,1,0:T(8,128)(2,1)}, bf16[6,64,256]{2,1,0:T(8,128)(2,1)S(1)}, u32[]{:S(2)}) copy-start(bf16[6,64,256]{2,1,0:T(8,128)(2,1)S(1)} %convolution_convert_fusion.22) | copy-start | bytes 589828
  294.9 64.8 %all-to-all-start = ((bf16[16,50,1152]{2,1,0:T(8,128)(2,1)}), bf16[16,50,1152]{2,1,0:T(8,128)(2,1)S(1)}, u32[]{:S(2)}, u32[]{:S(2)}) async-start(bf16[16,50,1152]{2,1,0:T(8,128)(2,1)} %pad_maximum_fusion.2), calls=%async_computation | async-start | bytes 4128768 | tf_op jit(solution)/shard_map/all_to_all | solution.py:292
  303.0 194.7 %reduce-scatter.2.cloned.1.call-start = ((), (), s32[]{:S(2)}) async-start(), calls=%async_computation.3 | async-start | bytes 5013504 | tf_op jit(solution)/shard_map/reduce_scatter | solution.py:356
  308.2 71.5 %copy-start.58 = (bf16[6,64,1024]{2,1,0:T(8,128)(2,1)S(1)}, bf16[6,64,1024]{2,1,0:T(8,128)(2,1)}, u32[]{:S(2)}) copy-start(bf16[6,64,1024]{2,1,0:T(8,128)(2,1)} %copy-done.57) | copy-start | bytes 2359300
  361.0 140.2 %all-to-all-start.1 = ((bf16[16,58,1920]{2,1,0:T(8,128)(2,1)}), bf16[16,58,1920]{2,1,0:T(8,128)(2,1)}, u32[]{:S(2)}, u32[]{:S(2)}) async-start(bf16[16,58,1920]{2,1,0:T(8,128)(2,1)} %pad_maximum_fusion.1), calls=%async_computation.1 | async-start | bytes 7864320 | tf_op jit(solution)/shard_map/all_to_all | solution.py:292
  383.1 7.9 %collective-permute-start.11 = (bf16[512,768]{0,1:T(8,128)(2,1)S(1)}, bf16[512,768]{0,1:T(8,128)(2,1)}, u32[]{:S(2)}, u32[]{:S(2)}) collective-permute-start(bf16[512,768]{0,1:T(8,128)(2,1)S(1)} %broadcast_select_fusion), channel_id=1, source_target_pairs={{0,1},{1,0},{2,3},{3,2},{4,5},{5,4},{6,7},{7,6},{8,9},{9,8},{10,11... | collective-permute-start | bytes 2359304 | tf_op jit(solution)/shard_map/ppermute | solution.py:158
  387.3 9.9 %collective-permute-start.10 = (bf16[512,768]{0,1:T(8,128)(2,1)S(1)}, bf16[512,768]{0,1:T(8,128)(2,1)}, u32[]{:S(2)}, u32[]{:S(2)}) collective-permute-start(bf16[512,768]{0,1:T(8,128)(2,1)S(1)} %broadcast_select_fusion.1), channel_id=1, source_target_pairs={{0,1},{1,0},{2,3},{3,2},{4,5},{5,4},{6,7},{7,6},{8,9},{9,8},{10,11... | collective-permute-start | bytes 2359304 | tf_op jit(solution)/shard_map/ppermute | solution.py:158
  390.9 6.2 %copy-start.19 = (f32[512,768]{0,1:T(8,128)S(1)}, f32[512,768]{0,1:T(8,128)}, u32[]{:S(2)}) copy-start(f32[512,768]{0,1:T(8,128)} %copy-done.18) | copy-start | bytes 4718596
  390.9 6.2 %copy-start.154 = (f32[512]{0:T(512)S(1)}, f32[512]{0:T(512)}, u32[]{:S(2)}) copy-start(f32[512]{0:T(512)} %copy-done.153) | copy-start | bytes 6148
  498.7 7.9 %copy-start.1 = (bf16[768,1536]{1,0:T(8,128)(2,1)S(1)}, bf16[768,1536]{1,0:T(8,128)(2,1)}, u32[]{:S(2)}) copy-start(bf16[768,1536]{1,0:T(8,128)(2,1)} %param.88) | copy-start | bytes 7077892
  (159 other events, 400.9 us)
Sparse Core Ops, SparseCore 0:
  309.0 188.6 reduce-scatter.1

commit v2 on v0

--- a/solution.py
+++ b/solution.py
@@ -334,52 +334,60 @@
     norm_pairs = sum_pair(
         jnp.concatenate([grad_first_gain, grad_first_shift, grad_second_gain, grad_second_shift])
     )
-    vector = jnp.concatenate(
-        [
-            grad_self_query_bias,
-            grad_self_value_bias,
-            grad_self_output_bias,
-            grad_cross_query_bias,
-            grad_cross_value_bias,
-            grad_cross_output_bias,
-            norm_pairs,
-            grad_third_gain,
-            grad_third_shift,
-            grad_inner_bias,
-            grad_outer_bias,
-        ]
-    )
     width = late_joined.shape[1]
-    lines = -(-vector.shape[0] // width)
-    padded = jnp.pad(vector, (0, lines * width - vector.shape[0])).reshape(lines, width)
-    high = padded.astype(jnp.bfloat16)
-    low = (padded - high.astype(jnp.float32)).astype(jnp.bfloat16)
-    late_rows = late_joined.shape[0] // dp_size
-    late_total = exchange_sum(late_joined, jnp.concatenate([high, low], 0))
-    self_sums = split_columns(late_total[:late_rows], late, (3,))
-    total = (
-        late_total[late_rows : late_rows + lines] + late_total[late_rows + lines :]
-    ).reshape(-1)
-    smalls = []
-    offset = 0
-    for piece in (
+    sections = norm_pairs.shape[0] // 4
+    biases = [
         grad_self_query_bias,
         grad_self_value_bias,
         grad_self_output_bias,
         grad_cross_query_bias,
         grad_cross_value_bias,
         grad_cross_output_bias,
-        grad_first_gain,
-        grad_first_shift,
-        grad_second_gain,
-        grad_second_shift,
+        norm_pairs[:sections],
+        norm_pairs[sections : 2 * sections],
+        norm_pairs[2 * sections : 3 * sections],
+        norm_pairs[3 * sections :],
         grad_third_gain,
         grad_third_shift,
         grad_inner_bias,
         grad_outer_bias,
-    ):
-        smalls.append(total[offset : offset + piece.shape[0]])
-        offset += piece.shape[0]
+    ]
+    lines = []
+    current = []
+    used = 0
+    places = []
+    for bias in biases:
+        chunks = []
+        for begin in range(0, bias.shape[0], width):
+            chunk = bias[begin : begin + width]
+            if used + chunk.shape[0] > width:
+                if used < width:
+                    current.append(jnp.zeros((width - used,), jnp.float32))
+                lines.append(jnp.concatenate(current))
+                current = []
+                used = 0
+            chunks.append((len(lines), used, chunk.shape[0]))
+            current.append(chunk)
+            used += chunk.shape[0]
+        places.append(chunks)
+    if used < width:
+        current.append(jnp.zeros((width - used,), jnp.float32))
+    lines.append(jnp.concatenate(current))
+    padded = jnp.stack(lines)
+    count = padded.shape[0]
+    high = padded.astype(jnp.bfloat16)
+    low = (padded - high.astype(jnp.float32)).astype(jnp.bfloat16)
+    late_rows = late_joined.shape[0] // dp_size
+    late_total = exchange_sum(late_joined, jnp.concatenate([high, low], 0))
+    self_sums = split_columns(late_total[:late_rows], late, (3,))
+    summed_lines = late_total[late_rows : late_rows + count] + late_total[late_rows + count :]
+    smalls = []
+    for chunks in places:
+        smalls.append(
+            jnp.concatenate(
+                [summed_lines[line, begin : begin + size] for line, begin, size in chunks]
+            )
+        )
     return (
         output,
         grad_tokens,

time: 433 us -> 422 us (0.975)
  waiting for transfers between devices: 49.9 us -> 73.7 us
  matrix products: 168 us -> 153 us
  local copies, waits for them, and re-layouts: 78.8 us -> 65 us
    all_to_all x2, waiting for transfers between devices: 44.4 us -> 67.6 us  [exchange_sum(): received = lax.all_to_all(blocks, 'dp', 0, 0, tiled=True)]
    dot_general x6, matrix products: 18.9 us -> 5.24 us  [attend_backward(): jnp.einsum('hqk,qhe->khe', grad_scores, piece, preferred_element_type=jnp...]
    unnamed x402 -> x395, local copies, waits for them, and re-layouts: 40.8 us -> 30.9 us
    another operation x0 -> x8, local copies, waits for them, and re-layouts: none -> 5.65 us  [on_device(): padded = jnp.stack(lines)]
  transfers between devices with their start and end apart: 15 -> 15, of which waited for: 4 -> 6; matrix products, arithmetic and copies ran while one was open for 50% -> 44% of each run, Pallas kernels for 0% -> 0%
where the time goes in v2:
time: 422 us; the launch traced here: 416 us
  matrix products  153 us (36%)
  other arithmetic  92.2 us (22%)
  waiting for transfers between devices  73.7 us (17%)
  local copies, waits for them, and re-layouts  65 us (15%)
  between operations  17 us (4%)
  starting transfers between devices  15.8 us (4%)
    dot_general x30, matrix products, project(): return jnp.dot(data, weight, preferred_element_type=jnp.float32)  69 us
    all_to_all x2, waiting for transfers between devices, exchange_sum(): received = lax.all_to_all(blocks, 'dp', 0, 0, tiled=True)  67.6 us
    unnamed x395, local copies, waits for them, and re-layouts  30.9 us
    dot_general x6, matrix products, attend_backward(): jnp.einsum('qhe,khe->hqk', grad_piece, values[:end], preferred_element_ty...  30 us
    convert_element_type x5, other arithmetic, attend_backward(): grad_scores = (probs * (grad_probs - row_inner)).astype(jnp.bfloat16)  28.1 us
    dot_general x6, matrix products, attend_backward(): jnp.einsum('hqk,qhe->khe', probs.astype(jnp.bfloat16), grad_piece, prefer...  14.6 us
    dot_general x6, matrix products, attend_forward(): jnp.einsum('hqk,khe->qhe', weights, values[:end], preferred_element_type=...  14.5 us
    all_to_all x2, starting transfers between devices, exchange_sum(): received = lax.all_to_all(blocks, 'dp', 0, 0, tiled=True)  12.7 us
  transfers between devices with their start and end apart: 15, of which 6 were waited for; matrix products, arithmetic and copies ran while one was open for 44% of the time, Pallas kernels for 0%

profile of v2, /device:TPU:12, one launch (start us, length us, event | category | flops | bytes accessed | tf_op | source)
XLA Modules:
  0.0 416.4 jit_solution(2527573026548606399)
XLA Ops:
  12.4 2.5 add_convert_fusion.8
  21.5 2.4 multiply_convert_fusion.8
  35.0 1.7 fusion.90
  37.9 1.6 fusion.22
  40.5 2.3 fusion.92
  44.0 1.6 copy-done.13
  50.9 2.9 fusion.153
  59.4 2.1 select_reduce_fusion
  61.5 3.4 fusion.1
  66.1 4.5 %fusion.88 = bf16[512,6,64]{0,2,1:T(8,128)(2,1)S(1)} fusion(bf16[1024,6,64]{0,2,1:T(8,128)(2,1)S(1)} %bitcast.261, f32[6,512,1024]{2,1,0:T(8,128)S(1)} %get-tuple-element.365, f32[6,512]{1,0:T(8,128)S(1)} %fusion.1, f32[6,512]{1,0:T(8,128)S(1)} %get-tuple-element.364, pred[512,1024]{1,0:T(8,128)(4,1)S(1)} %get-tuple-element.349), kind=kOutput, calls=%fused_computation.192 | convolution fusion | flops 415432704 | bytes 14311424 | tf_op jit(solution)/shard_map/hqk,khe->qhe/dot_general | solution.py:64
  70.7 2.1 select_reduce_fusion.1
  72.8 3.4 fusion
  77.4 4.1 fusion.87
  83.1 2.1 collective-permute-done.2
  86.7 2.1 collective-permute-done.3
  89.3 18.2 %multiply_convert_fusion.3 = (bf16[1024,1536]{1,0:T(8,128)(2,1)S(1)}, f32[1024,1536]{1,0:T(8,128)}, f32[1024,1536]{1,0:T(8,128)}) fusion(f32[1536]{0:T(1024)S(1)} %convert_element_type.329, bf16[768,1536]{1,0:T(8,128)(2,1)S(1)} %copy-done, bf16[512,768]{0,1:T(8,128)(2,1)S(1)} %get-tuple-element.325, bf16[512,768]{0,1:T(8,128)(2,1)S(1)} %get-tuple-element.324), kind=kOutput, calls=%fused_computation.28 | convolution fusion | flops 2522873856 | bytes 19666944 | tf_op jit(solution)/shard_map/dot_general | solution.py:22
  107.6 3.8 convolution_convert_fusion.5
  111.5 1.7 copy.98
  113.3 2.7 copy.84
  116.0 1.7 copy.99
  117.8 1.8 copy.100
  119.5 1.7 copy.101
  124.4 3.2 fusion.150
  130.0 2.7 convert_reduce_fusion.4
  132.7 6.9 %convert_reduce_fusion.1 = (f32[1536]{0:T(1024)S(1)}, bf16[1024,1536]{1,0:T(8,128)(2,1)S(1)}) fusion(f32[1024,1536]{1,0:T(8,128)S(1)} %bitcast.329, bf16[1536,768]{1,0:T(8,128)(2,1)S(1)} %copy-done.168, f32[1024,768]{0,1:T(8,128)S(1)} %get-tuple-element.304, f32[1024,1536]{1,0:T(8,128)} %get-tuple-element.368, f32[1536]{0:T(1024)S(1)} %copy-done.151), kind=kOutput, calls=%fused_computation.21 | convolution fusion | flops 2443442688 | bytes 21245952 | tf_op jit(solution)/shard_map/dot_general | solution.py:22
  139.7 2.6 convolution_convert_fusion.4
  144.7 2.8 convolution_convert_fusion
  151.9 3.0 convolution_convert_fusion.1
  154.9 2.7 pad_maximum_fusion
  161.5 6.4 %fusion.4 = f32[6,64,1024]{2,1,0:T(8,128)S(1)} fusion(bf16[512,6,64]{0,2,1:T(8,128)(2,1)S(1)} %bitcast.259, f32[6,512,1024]{2,1,0:T(8,128)} %copy-done.3, f32[6,512]{1,0:T(8,128)S(1)} %log_add_fusion, pred[512,1024]{1,0:T(8,128)(4,1)S(1)} %get-tuple-element.349), kind=kOutput, calls=%fused_computation.17 | convolution fusion | flops 412090368 | bytes 15085568 | tf_op jit(solution)/shard_map/hqk,qhe->khe/dot_general | solution.py:101
  167.9 9.8 %multiply_reduce_fusion = (f32[6,512]{1,0:T(8,128)S(1)}, f32[6,512,1024]{2,1,0:T(8,128)}) fusion(f32[6,512,1024]{2,1,0:T(8,128)} %copy-done.3, f32[6,512]{1,0:T(8,128)S(1)} %log_add_fusion, pred[512,1024]{1,0:T(8,128)(4,1)S(1)} %get-tuple-element.349, bf16[512,6,64]{0,2,1:T(8,128)(2,1)S(1)} %bitcast.260, bf16[1024,6,64]{0,2,1:T(8,128)(2,1)S(1)} %bitcast.263), kind=kOutput, calls=%fused_computation.1 | convolution fusion | flops 415233024 | bytes 26894336 | tf_op jit(solution)/shard_map/qhe,khe->hqk/dot_general | solution.py:89
  177.7 7.4 %multiply_reduce_fusion.1 = (f32[6,512]{1,0:T(8,128)S(1)}, f32[6,512,1024]{2,1,0:T(8,128)}) fusion(f32[6,512,1024]{2,1,0:T(8,128)S(1)} %bitcast.225, f32[6,512]{1,0:T(8,128)S(1)} %log_add_fusion.1, pred[512,1024]{1,0:T(8,128)(4,1)S(1)} %get-tuple-element.348, bf16[512,6,64]{0,2,1:T(8,128)(2,1)S(1)} %bitcast.257, bf16[1024,6,64]{0,2,1:T(8,128)(2,1)S(1)} %bitcast.264), kind=kOutput, calls=%fused_computation.4 | convolution fusion | flops 415233024 | bytes 26894336 | tf_op jit(solution)/shard_map/qhe,khe->hqk/dot_general | solution.py:89
  185.0 18.8 %multiply_convert_fusion = (bf16[6,512,1024]{2,1,0:T(8,128)(2,1)}, bf16[6,512,1024]{2,1,0:T(8,128)(2,1)}) fusion(f32[6,512,1024]{2,1,0:T(8,128)} %get-tuple-element.372, f32[6,512,1024]{2,1,0:T(8,128)} %copy-done.3, f32[6,512]{1,0:T(8,128)S(1)} %get-tuple-element.371, f32[6,512]{1,0:T(8,128)S(1)} %log_add_fusion, pred[512,1024]{1,0:T(8,128)(4,1)S(1)} %get-tuple-element.349, ...), kind=kLoop, calls=%fused_computation | loop fusion | flops 31457280 | bytes 64012288 | tf_op jit(solution)/shard_map/convert_element_type | solution.py:93
  203.9 5.0 %convolution_convert_fusion.19 = bf16[6,64,512]{2,1,0:T(8,128)(2,1)S(1)} fusion(bf16[1024,6,64]{0,2,1:T(8,128)(2,1)S(1)} %bitcast.240, bf16[6,512,1024]{2,1,0:T(8,128)(2,1)} %get-tuple-element.388), kind=kOutput, calls=%fused_computation.186 | convolution fusion | flops 402849792 | bytes 7471104 | tf_op jit(solution)/shard_map/hqk,khe->qhe/dot_general | solution.py:95
  210.2 4.0 convert_reduce_fusion.7
  214.2 1.6 fusion.81
  215.8 2.0 convolution_convert_fusion.18
  222.1 1.7 convolution_convert_fusion.14
  223.9 2.4 convolution_convert_fusion.17
  230.8 2.4 multiply_reduce_fusion.7
  243.0 2.4 copy.102
  245.5 7.4 %all-to-all-start.1 = ((bf16[16,48,1536]{2,1,0:T(8,128)(2,1)}), bf16[16,48,1536]{2,1,0:T(8,128)(2,1)}, u32[]{:S(2)}, u32[]{:S(2)}) async-start(bf16[16,48,1536]{2,1,0:T(8,128)(2,1)} %bitcast.71), calls=%async_computation.1 | async-start | bytes 4718592 | tf_op jit(solution)/shard_map/all_to_all | solution.py:323
  253.1 4.8 %multiply_reduce_fusion.4 = (f32[6,256]{1,0:T(8,128)S(1)}, f32[6,256,512]{2,1,0:T(8,128)}) fusion(f32[6,256,512]{2,1,0:T(8,128)} %copy-done.6, f32[6,256]{1,0:T(8,128)S(1)} %copy-done.127, pred[256,512]{1,0:T(8,128)(4,1)S(1)} %copy-done.45, bf16[512,6,64]{0,2,1:T(8,128)(2,1)} %bitcast.313, bf16[1024,6,64]{0,2,1:T(8,128)(2,1)S(1)} %bitcast.271), kind=kOutput, calls=%fused_computation.81 | convolution fusion | flops 103807488 | bytes 7026688 | tf_op jit(solution)/shard_map/qhe,khe->hqk/dot_general | solution.py:89
  259.2 3.6 multiply_reduce_fusion.3
  264.3 4.0 multiply_reduce_fusion.2
  268.3 1.6 convert_reduce_fusion.9
  270.0 2.4 fusion.84
  273.7 3.4 multiply_convert_fusion.5
  277.9 3.6 multiply_convert_fusion.4
  283.7 1.8 multiply_convert_fusion.2
  291.4 3.2 fusion.82
  294.7 2.2 copy.95
  300.7 1.8 pad_maximum_fusion.1
  302.5 23.1 %all-to-all-done.1 = bf16[16,48,1536]{2,1,0:T(8,128)(2,1)} async-done(((bf16[16,48,1536]{2,1,0:T(8,128)(2,1)}), bf16[16,48,1536]{2,1,0:T(8,128)(2,1)}, u32[]{:S(2)}, u32[]{:S(2)}) %all-to-all-start.1) | async-done | bytes 2359328 | tf_op jit(solution)/shard_map/all_to_all | solution.py:323
  325.6 5.3 %all-to-all-start = ((bf16[16,62,1536]{2,1,0:T(8,128)(2,1)}), bf16[16,62,1536]{2,1,0:T(8,128)(2,1)}, u32[]{:S(2)}, u32[]{:S(2)}) async-start(bf16[16,62,1536]{2,1,0:T(8,128)(2,1)} %pad_maximum_fusion.1), calls=%async_computation | async-start | bytes 6291456 | tf_op jit(solution)/shard_map/all_to_all | solution.py:323
  338.8 2.6 copy.103
  341.4 3.2 convert_add_fusion
  344.6 3.0 copy.105
  347.6 3.0 add_add_fusion.4
  350.6 3.0 copy.104
  353.6 2.0 convert_reduce_fusion.3
  356.4 44.5 %all-to-all-done = bf16[16,62,1536]{2,1,0:T(8,128)(2,1)} async-done(((bf16[16,62,1536]{2,1,0:T(8,128)(2,1)}), bf16[16,62,1536]{2,1,0:T(8,128)(2,1)}, u32[]{:S(2)}, u32[]{:S(2)}) %all-to-all-start) | async-done | bytes 3047456 | tf_op jit(solution)/shard_map/all_to_all | solution.py:323
  400.9 2.4 convert_reduce_fusion
  407.7 1.6 slice.648
  (577 shorter events, 107.3 us)
Async XLA Ops:
  7.2 82.1 %copy-start = (bf16[768,1536]{1,0:T(8,128)(2,1)S(1)}, bf16[768,1536]{1,0:T(8,128)(2,1)}, u32[]{:S(2)}) copy-start(bf16[768,1536]{1,0:T(8,128)(2,1)} %param.88) | copy-start | bytes 7077892
  7.2 398.7 %reduce-scatter.2.cloned.1.call-start = ((), (), s32[]{:S(2)}) async-start(), calls=%async_computation.3 | async-start | bytes 5013504 | tf_op jit(solution)/shard_map/reduce_scatter | solution.py:327
  18.2 18.4 %copy-start.26 = (bf16[1024,384]{0,1:T(8,128)(2,1)}, bf16[1024,384]{0,1:T(8,128)(2,1)S(1)}, u32[]{:S(2)}) copy-start(bf16[1024,384]{0,1:T(8,128)(2,1)S(1)} %convolution_convert_fusion.9) | copy-start | bytes 2359300
  19.1 9.8 %copy-start.52 = (bf16[512,384]{0,1:T(8,128)(2,1)}, bf16[512,384]{0,1:T(8,128)(2,1)S(1)}, u32[]{:S(2)}) copy-start(bf16[512,384]{0,1:T(8,128)(2,1)S(1)} %slice.603) | copy-start | bytes 1179652
  25.9 13.7 %copy-start.28 = (pred[256,1024]{1,0:T(8,128)(4,1)}, pred[256,1024]{1,0:T(8,128)(4,1)S(1)}, u32[]{:S(2)}) copy-start(pred[256,1024]{1,0:T(8,128)(4,1)S(1)} %fusion.93) | copy-start | bytes 786436
  28.7 14.2 %copy-start.99 = (bf16[6,64,256]{2,1,0:T(8,128)(2,1)}, bf16[6,64,256]{2,1,0:T(8,128)(2,1)S(1)}, u32[]{:S(2)}) copy-start(bf16[6,64,256]{2,1,0:T(8,128)(2,1)S(1)} %convolution_convert_fusion.24) | copy-start | bytes 589828
  32.2 10.7 %copy-start.100 = (bf16[6,64,256]{2,1,0:T(8,128)(2,1)}, bf16[6,64,256]{2,1,0:T(8,128)(2,1)S(1)}, u32[]{:S(2)}) copy-start(bf16[6,64,256]{2,1,0:T(8,128)(2,1)S(1)} %fusion.91) | copy-start | bytes 589828
  36.7 6.2 %copy-start.101 = (bf16[6,64,256]{2,1,0:T(8,128)(2,1)}, bf16[6,64,256]{2,1,0:T(8,128)(2,1)S(1)}, u32[]{:S(2)}) copy-start(bf16[6,64,256]{2,1,0:T(8,128)(2,1)S(1)} %fusion.90) | copy-start | bytes 589828
  47.2 3.8 collective-permute-start
  47.2 37.9 %copy-start.123 = (f32[768]{0:T(1024)}, f32[768]{0:T(1024)S(1)}, u32[]{:S(2)}) copy-start(f32[768]{0:T(1024)S(1)} %convert_element_type.310) | copy-start | bytes 9220
  53.8 31.3 %copy-start.8 = (f32[512,768]{0,1:T(8,128)}, f32[512,768]{0,1:T(8,128)S(1)}, u32[]{:S(2)}) copy-start(f32[512,768]{0,1:T(8,128)S(1)} %get-tuple-element.318) | copy-start | bytes 4718596
  53.9 31.3 %copy-start.130 = (f32[512]{0:T(512)}, f32[512]{0:T(512)S(1)}, u32[]{:S(2)}) copy-start(f32[512]{0:T(512)S(1)} %broadcast_multiply_fusion.2) | copy-start | bytes 6148
  54.2 31.0 %copy-start.132 = (f32[512]{0:T(512)}, f32[512]{0:T(512)S(1)}, u32[]{:S(2)}) copy-start(f32[512]{0:T(512)S(1)} %fusion.120) | copy-start | bytes 6148
  54.5 3.3 collective-permute-start.1
  56.9 13.8 %copy-start.24 = (bf16[1024,384]{0,1:T(8,128)(2,1)}, bf16[1024,384]{0,1:T(8,128)(2,1)S(1)}, u32[]{:S(2)}) copy-start(bf16[1024,384]{0,1:T(8,128)(2,1)S(1)} %convolution_convert_fusion.8) | copy-start | bytes 2359300
  57.8 18.4 %copy-start.54 = (bf16[1024,384]{0,1:T(8,128)(2,1)}, bf16[1024,384]{0,1:T(8,128)(2,1)S(1)}, u32[]{:S(2)}) copy-start(bf16[1024,384]{0,1:T(8,128)(2,1)S(1)} %add_convert_fusion.7) | copy-start | bytes 2359300
  59.4 11.3 %copy-start.48 = (bf16[512,384]{0,1:T(8,128)(2,1)}, bf16[512,384]{0,1:T(8,128)(2,1)S(1)}, u32[]{:S(2)}) copy-start(bf16[512,384]{0,1:T(8,128)(2,1)S(1)} %get-tuple-element.330) | copy-start | bytes 1179652
  82.8 2.4 collective-permute-start.2
  86.4 2.4 collective-permute-start.3
  86.7 20.9 %copy-start.150 = (f32[1536]{0:T(1024)}, f32[1536]{0:T(1024)S(1)}, u32[]{:S(2)}) copy-start(f32[1536]{0:T(1024)S(1)} %convert_element_type.329) | copy-start | bytes 18436
  89.3 18.2 %copy-start.58 = (bf16[512,768]{0,1:T(8,128)(2,1)}, bf16[512,768]{0,1:T(8,128)(2,1)S(1)}, u32[]{:S(2)}) copy-start(bf16[512,768]{0,1:T(8,128)(2,1)S(1)} %get-tuple-element.324) | copy-start | bytes 2359300
  89.3 18.2 %copy-start.60 = (bf16[512,768]{0,1:T(8,128)(2,1)}, bf16[512,768]{0,1:T(8,128)(2,1)S(1)}, u32[]{:S(2)}) copy-start(bf16[512,768]{0,1:T(8,128)(2,1)S(1)} %get-tuple-element.325) | copy-start | bytes 2359300
  89.3 18.2 %copy-start.167 = (bf16[1536,768]{1,0:T(8,128)(2,1)S(1)}, bf16[1536,768]{1,0:T(8,128)(2,1)}, u32[]{:S(2)}) copy-start(bf16[1536,768]{1,0:T(8,128)(2,1)} %param.90) | copy-start | bytes 7077892
  111.4 9.9 %copy-start.135 = (f32[6,256]{1,0:T(8,128)S(1)}, f32[6,256]{1,0:T(8,128)}, u32[]{:S(2)}) copy-start(f32[6,256]{1,0:T(8,128)} %copy-done.134) | copy-start | bytes 18436
  111.4 9.9 %copy-start.139 = (f32[6,256]{1,0:T(8,128)S(1)}, f32[6,256]{1,0:T(8,128)}, u32[]{:S(2)}) copy-start(f32[6,256]{1,0:T(8,128)} %copy-done.138) | copy-start | bytes 18436
  111.4 13.0 %collective-permute-start.4 = (bf16[1024,768]{0,1:T(8,128)(2,1)}, bf16[1024,768]{0,1:T(8,128)(2,1)}, u32[]{:S(2)}, u32[]{:S(2)}) collective-permute-start(bf16[1024,768]{0,1:T(8,128)(2,1)} %convolution_convert_fusion.5), channel_id=1, source_target_pairs={{0,1},{1,0},{2,3},{3,2},{4,5},{5,4},{6,7},{7,6},{8,9},{9,8},{10,11... | collective-permute-start | bytes 4718600 | tf_op jit(solution)/shard_map/ppermute | solution.py:158
  127.6 5.1 %slice-start.15 = ((s8[6291456]{0:T(1024)(128)(4,1)}), s8[4194304]{0:T(1024)(128)(4,1)S(1)}, s32[]{:S(2)}) async-start(s8[6291456]{0:T(1024)(128)(4,1)} %bitcast.328), calls=%async_computation.19 | async-start | bytes 8388608
  142.4 5.1 %collective-permute-start.5 = (bf16[512,768]{0,1:T(8,128)(2,1)S(1)}, bf16[512,768]{0,1:T(8,128)(2,1)S(1)}, u32[]{:S(2)}, u32[]{:S(2)}) collective-permute-start(bf16[512,768]{0,1:T(8,128)(2,1)S(1)} %broadcast_select_fusion.7), channel_id=1, source_target_pairs={{0,1},{1,0},{2,3},{3,2},{4,5},{5,4},{6,7},{7,6},{8,9},{9,8},{10,11... | collective-permute-start | bytes 2359304 | tf_op jit(solution)/shard_map/ppermute | solution.py:158
  149.6 8.1 %copy-start.141 = (f32[512]{0:T(512)}, f32[512]{0:T(512)S(1)}, u32[]{:S(2)}) copy-start(f32[512]{0:T(512)S(1)} %negate_multiply_fusion.3) | copy-start | bytes 6148
  151.8 5.9 %collective-permute-start.6 = (bf16[512,768]{0,1:T(8,128)(2,1)}, bf16[512,768]{0,1:T(8,128)(2,1)}, u32[]{:S(2)}, u32[]{:S(2)}) collective-permute-start(bf16[512,768]{0,1:T(8,128)(2,1)} %add_convert_fusion.10), channel_id=1, source_target_pairs={{0,1},{1,0},{2,3},{3,2},{4,5},{5,4},{6,7},{7,6},{8,9},{9,8},{10,11... | collective-permute-start | bytes 2359304 | tf_op jit(solution)/shard_map/ppermute | solution.py:158
  161.5 6.4 %copy-start.55 = (bf16[1024,384]{0,1:T(8,128)(2,1)S(1)}, bf16[1024,384]{0,1:T(8,128)(2,1)}, u32[]{:S(2)}) copy-start(bf16[1024,384]{0,1:T(8,128)(2,1)} %copy-done.54) | copy-start | bytes 2359300
  161.5 16.2 %slice-start = ((s8[12582912]{0:T(1024)(128)(4,1)}), s8[4194304]{0:T(1024)(128)(4,1)S(1)}, s32[]{:S(2)}) async-start(s8[12582912]{0:T(1024)(128)(4,1)} %bitcast.224), calls=%async_computation.4 | async-start | bytes 8388608
  161.5 16.2 %slice-start.1 = ((s8[12582912]{0:T(1024)(128)(4,1)}), s8[4194304]{0:T(1024)(128)(4,1)S(1)}, s32[]{:S(2)}) async-start(s8[12582912]{0:T(1024)(128)(4,1)} %bitcast.224), calls=%async_computation.5 | async-start | bytes 8388608
  167.9 9.8 %slice-start.2 = ((s8[12582912]{0:T(1024)(128)(4,1)}), s8[4194304]{0:T(1024)(128)(4,1)S(1)}, s32[]{:S(2)}) async-start(s8[12582912]{0:T(1024)(128)(4,1)} %bitcast.224), calls=%async_computation.6 | async-start | bytes 8388608
  185.0 18.8 %copy-start.25 = (bf16[1024,384]{0,1:T(8,128)(2,1)S(1)}, bf16[1024,384]{0,1:T(8,128)(2,1)}, u32[]{:S(2)}) copy-start(bf16[1024,384]{0,1:T(8,128)(2,1)} %copy-done.24) | copy-start | bytes 2359300
  208.9 6.9 %slice-start.11 = ((s8[6291456]{0:T(1024)(128)(4,1)}), s8[4194304]{0:T(1024)(128)(4,1)S(1)}, s32[]{:S(2)}) async-start(s8[6291456]{0:T(1024)(128)(4,1)} %bitcast.234), calls=%async_computation.15 | async-start | bytes 8388608
  210.2 5.6 %slice-start.12 = ((s8[6291456]{0:T(1024)(128)(4,1)}), s8[2097152]{0:T(1024)(128)(4,1)S(1)}, s32[]{:S(2)}) async-start(s8[6291456]{0:T(1024)(128)(4,1)} %bitcast.234), calls=%async_computation.16 | async-start | bytes 4194304
  219.1 7.2 %copy-start.50 = (bf16[6,64,1024]{2,1,0:T(8,128)(2,1)}, bf16[6,64,1024]{2,1,0:T(8,128)(2,1)S(1)}, u32[]{:S(2)}) copy-start(bf16[6,64,1024]{2,1,0:T(8,128)(2,1)S(1)} %add_convert_fusion.5) | copy-start | bytes 2359300
  221.3 7.9 %collective-permute-start.7 = (bf16[512,768]{0,1:T(8,128)(2,1)}, bf16[512,768]{0,1:T(8,128)(2,1)}, u32[]{:S(2)}, u32[]{:S(2)}) collective-permute-start(bf16[512,768]{0,1:T(8,128)(2,1)} %broadcast_select_fusion.4), channel_id=1, source_target_pairs={{0,1},{1,0},{2,3},{3,2},{4,5},{5,4},{6,7},{7,6},{8,9},{9,8},{10,11... | collective-permute-start | bytes 2359304 | tf_op jit(solution)/shard_map/ppermute | solution.py:158
  233.9 3.6 collective-permute-start.8
  234.8 1.5 collective-permute-start.11
  245.4 7.6 %copy-start.45 = (pred[256,512]{1,0:T(8,128)(4,1)S(1)}, pred[256,512]{1,0:T(8,128)(4,1)}, u32[]{:S(2)}) copy-start(pred[256,512]{1,0:T(8,128)(4,1)} %copy-done.44) | copy-start | bytes 393220
  245.5 7.6 %copy-start.65 = (bf16[1024,384]{0,1:T(8,128)(2,1)S(1)}, bf16[1024,384]{0,1:T(8,128)(2,1)}, u32[]{:S(2)}) copy-start(bf16[1024,384]{0,1:T(8,128)(2,1)} %copy-done.64) | copy-start | bytes 2359300
  245.5 7.6 %copy-start.127 = (f32[6,256]{1,0:T(8,128)S(1)}, f32[6,256]{1,0:T(8,128)}, u32[]{:S(2)}) copy-start(f32[6,256]{1,0:T(8,128)} %log_add_fusion.4) | copy-start | bytes 18436
  245.5 13.4 %slice-start.7 = ((s8[4718592]{0:T(1024)(128)(4,1)}), s8[524288]{0:T(1024)(128)(4,1)S(1)}, s32[]{:S(2)}) async-start(s8[4718592]{0:T(1024)(128)(4,1)} %bitcast.230), calls=%async_computation.11 | async-start | bytes 1048576
  245.5 80.2 %all-to-all-start.1 = ((bf16[16,48,1536]{2,1,0:T(8,128)(2,1)}), bf16[16,48,1536]{2,1,0:T(8,128)(2,1)}, u32[]{:S(2)}, u32[]{:S(2)}) async-start(bf16[16,48,1536]{2,1,0:T(8,128)(2,1)} %bitcast.71), calls=%async_computation.1 | async-start | bytes 4718592 | tf_op jit(solution)/shard_map/all_to_all | solution.py:323
  252.9 5.1 %copy-start.7 = (f32[6,256,512]{2,1,0:T(8,128)S(1)}, f32[6,256,512]{2,1,0:T(8,128)}, u32[]{:S(2)}) copy-start(f32[6,256,512]{2,1,0:T(8,128)} %copy-done.6) | copy-start | bytes 9437188
  253.1 5.8 %slice-start.8 = ((s8[4718592]{0:T(1024)(128)(4,1)}), s8[4194304]{0:T(1024)(128)(4,1)S(1)}, s32[]{:S(2)}) async-start(s8[4718592]{0:T(1024)(128)(4,1)} %bitcast.230), calls=%async_computation.12 | async-start | bytes 8388608
  257.9 6.3 %slice-start.3 = ((s8[6291456]{0:T(1024)(128)(4,1)}), s8[4194304]{0:T(1024)(128)(4,1)S(1)}, s32[]{:S(2)}) async-start(s8[6291456]{0:T(1024)(128)(4,1)} %bitcast.226), calls=%async_computation.7 | async-start | bytes 8388608
  270.0 7.2 %copy-start.53 = (bf16[512,384]{0,1:T(8,128)(2,1)S(1)}, bf16[512,384]{0,1:T(8,128)(2,1)}, u32[]{:S(2)}) copy-start(bf16[512,384]{0,1:T(8,128)(2,1)} %copy-done.52) | copy-start | bytes 1179652
  273.7 8.6 %slice-start.13 = ((s8[6291456]{0:T(1024)(128)(4,1)}), s8[4194304]{0:T(1024)(128)(4,1)S(1)}, s32[]{:S(2)}) async-start(s8[6291456]{0:T(1024)(128)(4,1)} %bitcast.236), calls=%async_computation.17 | async-start | bytes 8388608
  277.8 8.9 %copy-start.79 = (bf16[6,64,256]{2,1,0:T(8,128)(2,1)}, bf16[6,64,256]{2,1,0:T(8,128)(2,1)S(1)}, u32[]{:S(2)}) copy-start(bf16[6,64,256]{2,1,0:T(8,128)(2,1)S(1)} %convolution_convert_fusion.21) | copy-start | bytes 589828
  277.9 5.1 %slice-start.6 = ((s8[6291456]{0:T(1024)(128)(4,1)}), s8[2097152]{0:T(1024)(128)(4,1)S(1)}, s32[]{:S(2)}) async-start(s8[6291456]{0:T(1024)(128)(4,1)} %bitcast.228), calls=%async_computation.10 | async-start | bytes 4194304
  277.9 5.8 %slice-start.14 = ((s8[6291456]{0:T(1024)(128)(4,1)}), s8[2097152]{0:T(1024)(128)(4,1)S(1)}, s32[]{:S(2)}) async-start(s8[6291456]{0:T(1024)(128)(4,1)} %bitcast.236), calls=%async_computation.18 | async-start | bytes 4194304
  291.4 5.4 %copy-start.143 = (f32[1,1536]{1,0:T(1,128)S(1)}, f32[1,1536]{1,0:T(1,128)}, u32[]{:S(2)}) copy-start(f32[1,1536]{1,0:T(1,128)} %stack.28) | copy-start | bytes 18436
  291.4 6.9 %copy-start.34 = (bf16[512,768]{0,1:T(8,128)(2,1)S(1)}, bf16[512,768]{0,1:T(8,128)(2,1)}, u32[]{:S(2)}) copy-start(bf16[512,768]{0,1:T(8,128)(2,1)} %copy-done.33) | copy-start | bytes 2359300
  291.4 6.9 %copy-start.36 = (bf16[512,768]{0,1:T(8,128)(2,1)S(1)}, bf16[512,768]{0,1:T(8,128)(2,1)}, u32[]{:S(2)}) copy-start(bf16[512,768]{0,1:T(8,128)(2,1)} %copy-done.35) | copy-start | bytes 2359300
  302.5 28.4 %copy-start.51 = (bf16[6,64,1024]{2,1,0:T(8,128)(2,1)S(1)}, bf16[6,64,1024]{2,1,0:T(8,128)(2,1)}, u32[]{:S(2)}) copy-start(bf16[6,64,1024]{2,1,0:T(8,128)(2,1)} %copy-done.50) | copy-start | bytes 2359300
  302.5 28.4 %copy-start.108 = (bf16[768,384]{1,0:T(8,128)(2,1)S(1)}, bf16[768,384]{1,0:T(8,128)(2,1)}, u32[]{:S(2)}) copy-start(bf16[768,384]{1,0:T(8,128)(2,1)} %param.77) | copy-start | bytes 1769476
  325.6 75.2 %all-to-all-start = ((bf16[16,62,1536]{2,1,0:T(8,128)(2,1)}), bf16[16,62,1536]{2,1,0:T(8,128)(2,1)}, u32[]{:S(2)}, u32[]{:S(2)}) async-start(bf16[16,62,1536]{2,1,0:T(8,128)(2,1)} %pad_maximum_fusion.1), calls=%async_computation | async-start | bytes 6291456 | tf_op jit(solution)/shard_map/all_to_all | solution.py:323
  334.3 7.1 %collective-permute-start.10 = (bf16[512,768]{0,1:T(8,128)(2,1)}, bf16[512,768]{0,1:T(8,128)(2,1)}, u32[]{:S(2)}, u32[]{:S(2)}) collective-permute-start(bf16[512,768]{0,1:T(8,128)(2,1)} %broadcast_select_fusion), channel_id=1, source_target_pairs={{0,1},{1,0},{2,3},{3,2},{4,5},{5,4},{6,7},{7,6},{8,9},{9,8},{10,11... | collective-permute-start | bytes 2359304 | tf_op jit(solution)/shard_map/ppermute | solution.py:158
  337.8 9.9 %collective-permute-start.9 = (bf16[512,768]{0,1:T(8,128)(2,1)S(1)}, bf16[512,768]{0,1:T(8,128)(2,1)S(1)}, u32[]{:S(2)}, u32[]{:S(2)}) collective-permute-start(bf16[512,768]{0,1:T(8,128)(2,1)S(1)} %broadcast_select_fusion.1), channel_id=1, source_target_pairs={{0,1},{1,0},{2,3},{3,2},{4,5},{5,4},{6,7},{7,6},{8,9},{9,8},{10,11... | collective-permute-start | bytes 2359304 | tf_op jit(solution)/shard_map/ppermute | solution.py:158
  341.4 6.2 %copy-start.18 = (f32[512,768]{0,1:T(8,128)S(1)}, f32[512,768]{0,1:T(8,128)}, u32[]{:S(2)}) copy-start(f32[512,768]{0,1:T(8,128)} %copy-done.17) | copy-start | bytes 4718596
  355.7 53.6 %copy-start.1 = (bf16[768,1536]{1,0:T(8,128)(2,1)S(1)}, bf16[768,1536]{1,0:T(8,128)(2,1)}, u32[]{:S(2)}) copy-start(bf16[768,1536]{1,0:T(8,128)(2,1)} %param.88) | copy-start | bytes 7077892
  (146 other events, 336.3 us)
Sparse Core Ops, SparseCore 0:
  157.8 161.4 reduce-scatter.1

commit v3 on v2

--- a/solution.py
+++ b/solution.py
@@ -269,16 +269,16 @@
     grad_first = grad_second_in + scatter_rows(
         project(cross_grad_q, cross_query.T).astype(jnp.bfloat16)
     )
+    grad_cross_output_t = project(grad_cross.T, cross_context)
+    cross = [grad_cross_query, grad_cross_key, grad_cross_value, grad_cross_output_t]
+    cross_joined = jnp.concatenate(cross, 1).astype(jnp.bfloat16)
+    cross_joined, grad_first = lax.optimization_barrier((cross_joined, grad_first))
     grad_first_in, grad_first_gain, grad_first_shift = first_back(grad_first)
     grad_self_rows = grad_first_in.astype(jnp.bfloat16)
     grad_self = gather_rows(grad_self_rows)
     grad_self_output_bias = column_sums(grad_self)
     grad_self_context = heads_of(project(grad_self, self_output.T).astype(jnp.bfloat16))
     dp_size = lax.axis_size("dp")
-    grad_cross_output_t = project(grad_cross.T, cross_context)
-    cross = [grad_cross_query, grad_cross_key, grad_cross_value, grad_cross_output_t]
-    cross_joined = jnp.concatenate(cross, 1).astype(jnp.bfloat16)
-    cross_joined, grad_self_context = lax.optimization_barrier((cross_joined, grad_self_context))
     self_grad_q, self_grad_k, self_grad_v = attend_backward(
         self_queries, self_keys, self_values, grad_self_context, self_totals, segment, True
     )

time: 422 us -> 418 us (level)
  waiting for transfers between devices: 73.7 us -> 63.4 us
    all_to_all x2, waiting for transfers between devices: 67.6 us -> 57.8 us  [exchange_sum(): received = lax.all_to_all(blocks, 'dp', 0, 0, tiled=True)]
    unnamed x395 -> x413, local copies, waits for them, and re-layouts: 30.9 us -> 31 us
  transfers between devices with their start and end apart: 15 -> 15, of which waited for: 6 -> 5; matrix products, arithmetic and copies ran while one was open for 44% -> 45% of each run, Pallas kernels for 0% -> 0%
where the time goes in v3:
time: 418 us; the launch traced here: 412 us
  matrix products  153 us (37%)
  other arithmetic  94.4 us (23%)
  local copies, waits for them, and re-layouts  66.3 us (16%)
  waiting for transfers between devices  63.4 us (15%)
  between operations  17.2 us (4%)
  starting transfers between devices  16.7 us (4%)
    dot_general x30, matrix products, project(): return jnp.dot(data, weight, preferred_element_type=jnp.float32)  70.1 us
    all_to_all x2, waiting for transfers between devices, exchange_sum(): received = lax.all_to_all(blocks, 'dp', 0, 0, tiled=True)  57.8 us
    unnamed x413, local copies, waits for them, and re-layouts  31 us
    dot_general x6, matrix products, attend_backward(): jnp.einsum('qhe,khe->hqk', grad_piece, values[:end], preferred_element_ty...  30 us
    convert_element_type x5, other arithmetic, attend_backward(): grad_scores = (probs * (grad_probs - row_inner)).astype(jnp.bfloat16)  28.1 us
    dot_general x6, matrix products, attend_backward(): jnp.einsum('hqk,qhe->khe', probs.astype(jnp.bfloat16), grad_piece, prefer...  15 us
    dot_general x6, matrix products, attend_forward(): jnp.einsum('hqk,khe->qhe', weights, values[:end], preferred_element_type=...  14.5 us
    all_to_all x2, starting transfers between devices, exchange_sum(): received = lax.all_to_all(blocks, 'dp', 0, 0, tiled=True)  13.4 us
  transfers between devices with their start and end apart: 15, of which 5 were waited for; matrix products, arithmetic and copies ran while one was open for 45% of the time, Pallas kernels for 0%

profile of v3, /device:TPU:12, one launch (start us, length us, event | category | flops | bytes accessed | tf_op | source)
XLA Modules:
  0.0 411.5 jit_solution(13144595094908202876)
XLA Ops:
  12.4 2.5 add_convert_fusion.8
  21.4 2.4 multiply_convert_fusion.8
  34.9 1.7 fusion.90
  37.9 1.6 fusion.22
  40.4 2.3 fusion.92
  44.0 1.7 copy-done.13
  50.9 2.9 fusion.141
  59.4 2.1 select_reduce_fusion
  61.6 3.4 fusion.1
  66.1 4.5 %fusion.88 = bf16[512,6,64]{0,2,1:T(8,128)(2,1)S(1)} fusion(bf16[1024,6,64]{0,2,1:T(8,128)(2,1)S(1)} %bitcast.273, f32[6,512,1024]{2,1,0:T(8,128)S(1)} %get-tuple-element.368, f32[6,512]{1,0:T(8,128)S(1)} %fusion.1, f32[6,512]{1,0:T(8,128)S(1)} %get-tuple-element.367, pred[512,1024]{1,0:T(8,128)(4,1)S(1)} %get-tuple-element.352), kind=kOutput, calls=%fused_computation.192 | convolution fusion | flops 415432704 | bytes 14311424 | tf_op jit(solution)/shard_map/hqk,khe->qhe/dot_general | solution.py:64
  70.7 2.1 select_reduce_fusion.1
  72.8 3.4 fusion
  77.4 4.1 %fusion.87 = bf16[512,6,64]{0,2,1:T(8,128)(2,1)S(1)} fusion(bf16[1024,6,64]{0,2,1:T(8,128)(2,1)S(1)} %bitcast.274, f32[6,512,1024]{2,1,0:T(8,128)S(1)} %get-tuple-element.370, f32[6,512]{1,0:T(8,128)S(1)} %fusion, f32[6,512]{1,0:T(8,128)S(1)} %get-tuple-element.369, pred[512,1024]{1,0:T(8,128)(4,1)S(1)} %get-tuple-element.351), kind=kOutput, calls=%fused_computation.191 | convolution fusion | flops 415432704 | bytes 14311424 | tf_op jit(solution)/shard_map/hqk,khe->qhe/dot_general | solution.py:64
  83.1 2.1 collective-permute-done.2
  86.7 2.1 collective-permute-done.3
  89.3 18.2 %multiply_convert_fusion.3 = (bf16[1024,1536]{1,0:T(8,128)(2,1)S(1)}, f32[1024,1536]{1,0:T(8,128)}, f32[1024,1536]{1,0:T(8,128)}) fusion(f32[1536]{0:T(1024)S(1)} %convert_element_type.329, bf16[768,1536]{1,0:T(8,128)(2,1)S(1)} %copy-done, bf16[512,768]{0,1:T(8,128)(2,1)S(1)} %get-tuple-element.324, bf16[512,768]{0,1:T(8,128)(2,1)S(1)} %get-tuple-element.323), kind=kOutput, calls=%fused_computation.28 | convolution fusion | flops 2522873856 | bytes 19666944 | tf_op jit(solution)/shard_map/dot_general | solution.py:22
  107.6 3.8 convolution_convert_fusion.5
  111.5 1.8 copy.94
  113.3 2.7 copy.80
  116.0 1.8 copy.95
  117.8 1.7 copy.96
  119.5 1.8 copy.97
  124.4 3.2 fusion.138
  130.0 2.7 convert_reduce_fusion.4
  132.7 7.0 %convert_reduce_fusion.1 = (f32[1536]{0:T(1024)S(1)}, bf16[1024,1536]{1,0:T(8,128)(2,1)S(1)}) fusion(f32[1024,1536]{1,0:T(8,128)S(1)} %bitcast.341, bf16[1536,768]{1,0:T(8,128)(2,1)S(1)} %copy-done.178, f32[1024,768]{0,1:T(8,128)S(1)} %get-tuple-element.304, f32[1024,1536]{1,0:T(8,128)} %get-tuple-element.371, f32[1536]{0:T(1024)S(1)} %copy-done.159), kind=kOutput, calls=%fused_computation.21 | convolution fusion | flops 2443442688 | bytes 21245952 | tf_op jit(solution)/shard_map/dot_general | solution.py:22
  139.7 2.6 convolution_convert_fusion.4
  144.7 2.8 convolution_convert_fusion
  152.0 3.0 convolution_convert_fusion.1
  155.0 2.7 pad_maximum_fusion
  161.6 6.4 %fusion.4 = f32[6,64,1024]{2,1,0:T(8,128)S(1)} fusion(bf16[512,6,64]{0,2,1:T(8,128)(2,1)S(1)} %bitcast.271, f32[6,512,1024]{2,1,0:T(8,128)} %copy-done.3, f32[6,512]{1,0:T(8,128)S(1)} %log_add_fusion, pred[512,1024]{1,0:T(8,128)(4,1)S(1)} %get-tuple-element.352), kind=kOutput, calls=%fused_computation.17 | convolution fusion | flops 412090368 | bytes 15085568 | tf_op jit(solution)/shard_map/hqk,qhe->khe/dot_general | solution.py:101
  168.0 9.8 %multiply_reduce_fusion = (f32[6,512]{1,0:T(8,128)S(1)}, f32[6,512,1024]{2,1,0:T(8,128)}) fusion(f32[6,512,1024]{2,1,0:T(8,128)} %copy-done.3, f32[6,512]{1,0:T(8,128)S(1)} %log_add_fusion, pred[512,1024]{1,0:T(8,128)(4,1)S(1)} %get-tuple-element.352, bf16[512,6,64]{0,2,1:T(8,128)(2,1)S(1)} %bitcast.272, bf16[1024,6,64]{0,2,1:T(8,128)(2,1)S(1)} %bitcast.275), kind=kOutput, calls=%fused_computation.1 | convolution fusion | flops 415233024 | bytes 26894336 | tf_op jit(solution)/shard_map/qhe,khe->hqk/dot_general | solution.py:89
  177.8 7.2 %multiply_reduce_fusion.1 = (f32[6,512]{1,0:T(8,128)S(1)}, f32[6,512,1024]{2,1,0:T(8,128)}) fusion(f32[6,512,1024]{2,1,0:T(8,128)S(1)} %bitcast.236, f32[6,512]{1,0:T(8,128)S(1)} %log_add_fusion.1, pred[512,1024]{1,0:T(8,128)(4,1)S(1)} %get-tuple-element.351, bf16[512,6,64]{0,2,1:T(8,128)(2,1)S(1)} %bitcast.269, bf16[1024,6,64]{0,2,1:T(8,128)(2,1)S(1)} %bitcast.276), kind=kOutput, calls=%fused_computation.4 | convolution fusion | flops 415233024 | bytes 26894336 | tf_op jit(solution)/shard_map/qhe,khe->hqk/dot_general | solution.py:89
  185.0 18.7 %multiply_convert_fusion = (bf16[6,512,1024]{2,1,0:T(8,128)(2,1)}, bf16[6,512,1024]{2,1,0:T(8,128)(2,1)}) fusion(f32[6,512,1024]{2,1,0:T(8,128)} %get-tuple-element.375, f32[6,512,1024]{2,1,0:T(8,128)} %copy-done.3, f32[6,512]{1,0:T(8,128)S(1)} %get-tuple-element.374, f32[6,512]{1,0:T(8,128)S(1)} %log_add_fusion, pred[512,1024]{1,0:T(8,128)(4,1)S(1)} %get-tuple-element.352, ...), kind=kLoop, calls=%fused_computation | loop fusion | flops 31457280 | bytes 64012288 | tf_op jit(solution)/shard_map/convert_element_type | solution.py:93
  203.8 5.0 %convolution_convert_fusion.19 = bf16[6,64,512]{2,1,0:T(8,128)(2,1)S(1)} fusion(bf16[1024,6,64]{0,2,1:T(8,128)(2,1)S(1)} %bitcast.251, bf16[6,512,1024]{2,1,0:T(8,128)(2,1)} %get-tuple-element.391), kind=kOutput, calls=%fused_computation.186 | convolution fusion | flops 402849792 | bytes 7471104 | tf_op jit(solution)/shard_map/hqk,khe->qhe/dot_general | solution.py:95
  210.1 4.0 convert_reduce_fusion.7
  214.1 1.6 fusion.81
  215.8 2.0 convolution_convert_fusion.18
  222.1 1.6 convolution_convert_fusion.14
  224.3 2.3 convolution_convert_fusion.17
  226.7 2.3 fusion.80
  238.0 2.4 copy.98
  240.4 7.4 %all-to-all-start.1 = ((bf16[16,48,1536]{2,1,0:T(8,128)(2,1)}), bf16[16,48,1536]{2,1,0:T(8,128)(2,1)}, u32[]{:S(2)}, u32[]{:S(2)}) async-start(bf16[16,48,1536]{2,1,0:T(8,128)(2,1)} %bitcast.255), calls=%async_computation.1 | async-start | bytes 4718592 | tf_op jit(solution)/shard_map/all_to_all | solution.py:323
  256.6 3.4 multiply_reduce_fusion.4
  261.2 4.4 %multiply_reduce_fusion.3 = (f32[6,256]{1,0:T(8,128)}, f32[6,256,768]{2,1,0:T(8,128)}) fusion(f32[6,256,768]{2,1,0:T(8,128)S(1)} %bitcast.242, f32[6,256]{1,0:T(8,128)S(1)} %copy-done.127, pred[256,768]{1,0:T(8,128)(4,1)S(1)} %copy-done.33, bf16[256,6,64]{0,2,1:T(8,128)(2,1)S(1)} %bitcast.316, bf16[768,6,64]{0,2,1:T(8,128)(2,1)S(1)} %bitcast.284), kind=kOutput, calls=%fused_computation.59 | convolution fusion | flops 155712000 | bytes 10432512 | tf_op jit(solution)/shard_map/qhe,khe->hqk/dot_general | solution.py:89
  267.1 4.8 %multiply_reduce_fusion.2 = (f32[6,256]{1,0:T(8,128)}, f32[6,256,1024]{2,1,0:T(8,128)}) fusion(f32[6,256,1024]{2,1,0:T(8,128)S(1)} %bitcast.238, f32[6,256]{1,0:T(8,128)S(1)} %copy-done.125, pred[256,1024]{1,0:T(8,128)(4,1)S(1)} %copy-done.30, bf16[256,6,64]{0,2,1:T(8,128)(2,1)S(1)} %bitcast.314, bf16[1024,6,64]{0,2,1:T(8,128)(2,1)S(1)} %bitcast.260), kind=kOutput, calls=%fused_computation.23 | convolution fusion | flops 207616512 | bytes 13840384 | tf_op jit(solution)/shard_map/qhe,khe->hqk/dot_general | solution.py:89
  271.9 1.9 convert_reduce_fusion.9
  274.5 2.3 fusion.84
  278.1 3.5 multiply_convert_fusion.5
  282.3 3.8 multiply_convert_fusion.4
  288.0 1.6 multiply_convert_fusion.2
  295.5 3.2 fusion.82
  298.8 2.2 copy.91
  304.8 1.8 pad_maximum_fusion.1
  306.6 13.7 %all-to-all-done.1 = bf16[16,48,1536]{2,1,0:T(8,128)(2,1)} async-done(((bf16[16,48,1536]{2,1,0:T(8,128)(2,1)}), bf16[16,48,1536]{2,1,0:T(8,128)(2,1)}, u32[]{:S(2)}, u32[]{:S(2)}) %all-to-all-start.1) | async-done | bytes 2359328 | tf_op jit(solution)/shard_map/all_to_all | solution.py:323
  320.3 6.0 %all-to-all-start = ((bf16[16,62,1536]{2,1,0:T(8,128)(2,1)}), bf16[16,62,1536]{2,1,0:T(8,128)(2,1)}, u32[]{:S(2)}, u32[]{:S(2)}) async-start(bf16[16,62,1536]{2,1,0:T(8,128)(2,1)} %pad_maximum_fusion.1), calls=%async_computation | async-start | bytes 6291456 | tf_op jit(solution)/shard_map/all_to_all | solution.py:323
  334.3 2.6 copy.99
  336.8 3.2 convert_add_fusion
  340.0 3.0 copy.101
  343.1 3.0 add_add_fusion.4
  346.1 3.0 copy.100
  349.1 2.0 convert_reduce_fusion.3
  351.9 44.1 %all-to-all-done = bf16[16,62,1536]{2,1,0:T(8,128)(2,1)} async-done(((bf16[16,62,1536]{2,1,0:T(8,128)(2,1)}), bf16[16,62,1536]{2,1,0:T(8,128)(2,1)}, u32[]{:S(2)}, u32[]{:S(2)}) %all-to-all-start) | async-done | bytes 3047456 | tf_op jit(solution)/shard_map/all_to_all | solution.py:323
  396.0 2.4 convert_reduce_fusion
  402.7 1.6 slice.668
  (597 shorter events, 111.5 us)
Async XLA Ops:
  7.2 82.1 %copy-start = (bf16[768,1536]{1,0:T(8,128)(2,1)S(1)}, bf16[768,1536]{1,0:T(8,128)(2,1)}, u32[]{:S(2)}) copy-start(bf16[768,1536]{1,0:T(8,128)(2,1)} %param.88) | copy-start | bytes 7077892
  7.2 393.8 %reduce-scatter.2.cloned.1.call-start = ((), (), s32[]{:S(2)}) async-start(), calls=%async_computation.3 | async-start | bytes 5013504 | tf_op jit(solution)/shard_map/reduce_scatter | solution.py:327
  18.2 18.4 %copy-start.27 = (bf16[1024,384]{0,1:T(8,128)(2,1)}, bf16[1024,384]{0,1:T(8,128)(2,1)S(1)}, u32[]{:S(2)}) copy-start(bf16[1024,384]{0,1:T(8,128)(2,1)S(1)} %convolution_convert_fusion.9) | copy-start | bytes 2359300
  19.0 9.8 %copy-start.53 = (bf16[512,384]{0,1:T(8,128)(2,1)}, bf16[512,384]{0,1:T(8,128)(2,1)S(1)}, u32[]{:S(2)}) copy-start(bf16[512,384]{0,1:T(8,128)(2,1)S(1)} %slice.619) | copy-start | bytes 1179652
  25.8 13.7 %copy-start.29 = (pred[256,1024]{1,0:T(8,128)(4,1)}, pred[256,1024]{1,0:T(8,128)(4,1)S(1)}, u32[]{:S(2)}) copy-start(pred[256,1024]{1,0:T(8,128)(4,1)S(1)} %fusion.93) | copy-start | bytes 786436
  28.6 14.2 %copy-start.98 = (bf16[6,64,256]{2,1,0:T(8,128)(2,1)}, bf16[6,64,256]{2,1,0:T(8,128)(2,1)S(1)}, u32[]{:S(2)}) copy-start(bf16[6,64,256]{2,1,0:T(8,128)(2,1)S(1)} %convolution_convert_fusion.24) | copy-start | bytes 589828
  32.1 10.7 %copy-start.99 = (bf16[6,64,256]{2,1,0:T(8,128)(2,1)}, bf16[6,64,256]{2,1,0:T(8,128)(2,1)S(1)}, u32[]{:S(2)}) copy-start(bf16[6,64,256]{2,1,0:T(8,128)(2,1)S(1)} %fusion.91) | copy-start | bytes 589828
  36.6 6.2 %copy-start.100 = (bf16[6,64,256]{2,1,0:T(8,128)(2,1)}, bf16[6,64,256]{2,1,0:T(8,128)(2,1)S(1)}, u32[]{:S(2)}) copy-start(bf16[6,64,256]{2,1,0:T(8,128)(2,1)S(1)} %fusion.90) | copy-start | bytes 589828
  47.1 3.8 collective-permute-start
  47.2 38.0 %copy-start.122 = (f32[768]{0:T(1024)}, f32[768]{0:T(1024)S(1)}, u32[]{:S(2)}) copy-start(f32[768]{0:T(1024)S(1)} %convert_element_type.310) | copy-start | bytes 9220
  53.8 31.4 %copy-start.8 = (f32[512,768]{0,1:T(8,128)}, f32[512,768]{0,1:T(8,128)S(1)}, u32[]{:S(2)}) copy-start(f32[512,768]{0,1:T(8,128)S(1)} %get-tuple-element.317) | copy-start | bytes 4718596
  53.9 31.3 %copy-start.130 = (f32[512]{0:T(512)}, f32[512]{0:T(512)S(1)}, u32[]{:S(2)}) copy-start(f32[512]{0:T(512)S(1)} %broadcast_multiply_fusion.2) | copy-start | bytes 6148
  54.1 31.1 %copy-start.132 = (f32[512]{0:T(512)}, f32[512]{0:T(512)S(1)}, u32[]{:S(2)}) copy-start(f32[512]{0:T(512)S(1)} %fusion.108) | copy-start | bytes 6148
  54.5 3.3 collective-permute-start.1
  56.9 13.8 %copy-start.25 = (bf16[1024,384]{0,1:T(8,128)(2,1)}, bf16[1024,384]{0,1:T(8,128)(2,1)S(1)}, u32[]{:S(2)}) copy-start(bf16[1024,384]{0,1:T(8,128)(2,1)S(1)} %convolution_convert_fusion.8) | copy-start | bytes 2359300
  57.7 18.5 %copy-start.55 = (bf16[1024,384]{0,1:T(8,128)(2,1)}, bf16[1024,384]{0,1:T(8,128)(2,1)S(1)}, u32[]{:S(2)}) copy-start(bf16[1024,384]{0,1:T(8,128)(2,1)S(1)} %add_convert_fusion.7) | copy-start | bytes 2359300
  59.4 11.3 %copy-start.49 = (bf16[512,384]{0,1:T(8,128)(2,1)}, bf16[512,384]{0,1:T(8,128)(2,1)S(1)}, u32[]{:S(2)}) copy-start(bf16[512,384]{0,1:T(8,128)(2,1)S(1)} %get-tuple-element.333) | copy-start | bytes 1179652
  82.8 2.4 collective-permute-start.2
  86.5 2.4 collective-permute-start.3
  86.7 20.8 %copy-start.158 = (f32[1536]{0:T(1024)}, f32[1536]{0:T(1024)S(1)}, u32[]{:S(2)}) copy-start(f32[1536]{0:T(1024)S(1)} %convert_element_type.329) | copy-start | bytes 18436
  89.3 18.2 %copy-start.59 = (bf16[512,768]{0,1:T(8,128)(2,1)}, bf16[512,768]{0,1:T(8,128)(2,1)S(1)}, u32[]{:S(2)}) copy-start(bf16[512,768]{0,1:T(8,128)(2,1)S(1)} %get-tuple-element.323) | copy-start | bytes 2359300
  89.3 18.2 %copy-start.61 = (bf16[512,768]{0,1:T(8,128)(2,1)}, bf16[512,768]{0,1:T(8,128)(2,1)S(1)}, u32[]{:S(2)}) copy-start(bf16[512,768]{0,1:T(8,128)(2,1)S(1)} %get-tuple-element.324) | copy-start | bytes 2359300
  89.3 18.2 %copy-start.177 = (bf16[1536,768]{1,0:T(8,128)(2,1)S(1)}, bf16[1536,768]{1,0:T(8,128)(2,1)}, u32[]{:S(2)}) copy-start(bf16[1536,768]{1,0:T(8,128)(2,1)} %param.90) | copy-start | bytes 7077892
  111.3 9.9 %copy-start.135 = (f32[6,256]{1,0:T(8,128)S(1)}, f32[6,256]{1,0:T(8,128)}, u32[]{:S(2)}) copy-start(f32[6,256]{1,0:T(8,128)} %copy-done.134) | copy-start | bytes 18436
  111.3 9.9 %copy-start.139 = (f32[6,256]{1,0:T(8,128)S(1)}, f32[6,256]{1,0:T(8,128)}, u32[]{:S(2)}) copy-start(f32[6,256]{1,0:T(8,128)} %copy-done.138) | copy-start | bytes 18436
  111.3 13.1 %collective-permute-start.4 = (bf16[1024,768]{0,1:T(8,128)(2,1)}, bf16[1024,768]{0,1:T(8,128)(2,1)}, u32[]{:S(2)}, u32[]{:S(2)}) collective-permute-start(bf16[1024,768]{0,1:T(8,128)(2,1)} %convolution_convert_fusion.5), channel_id=1, source_target_pairs={{0,1},{1,0},{2,3},{3,2},{4,5},{5,4},{6,7},{7,6},{8,9},{9,8},{10,11... | collective-permute-start | bytes 4718600 | tf_op jit(solution)/shard_map/ppermute | solution.py:158
  142.4 5.1 %collective-permute-start.5 = (bf16[512,768]{0,1:T(8,128)(2,1)S(1)}, bf16[512,768]{0,1:T(8,128)(2,1)S(1)}, u32[]{:S(2)}, u32[]{:S(2)}) collective-permute-start(bf16[512,768]{0,1:T(8,128)(2,1)S(1)} %broadcast_select_fusion.7), channel_id=1, source_target_pairs={{0,1},{1,0},{2,3},{3,2},{4,5},{5,4},{6,7},{7,6},{8,9},{9,8},{10,11... | collective-permute-start | bytes 2359304 | tf_op jit(solution)/shard_map/ppermute | solution.py:158
  149.6 8.1 %copy-start.144 = (f32[512]{0:T(512)}, f32[512]{0:T(512)S(1)}, u32[]{:S(2)}) copy-start(f32[512]{0:T(512)S(1)} %negate_multiply_fusion.3) | copy-start | bytes 6148
  151.8 5.9 %collective-permute-start.6 = (bf16[512,768]{0,1:T(8,128)(2,1)}, bf16[512,768]{0,1:T(8,128)(2,1)}, u32[]{:S(2)}, u32[]{:S(2)}) collective-permute-start(bf16[512,768]{0,1:T(8,128)(2,1)} %add_convert_fusion.10), channel_id=1, source_target_pairs={{0,1},{1,0},{2,3},{3,2},{4,5},{5,4},{6,7},{7,6},{8,9},{9,8},{10,11... | collective-permute-start | bytes 2359304 | tf_op jit(solution)/shard_map/ppermute | solution.py:158
  161.6 6.4 %copy-start.56 = (bf16[1024,384]{0,1:T(8,128)(2,1)S(1)}, bf16[1024,384]{0,1:T(8,128)(2,1)}, u32[]{:S(2)}) copy-start(bf16[1024,384]{0,1:T(8,128)(2,1)} %copy-done.55) | copy-start | bytes 2359300
  161.6 16.2 %slice-start = ((s8[12582912]{0:T(1024)(128)(4,1)}), s8[4194304]{0:T(1024)(128)(4,1)S(1)}, s32[]{:S(2)}) async-start(s8[12582912]{0:T(1024)(128)(4,1)} %bitcast.235), calls=%async_computation.4 | async-start | bytes 8388608
  161.6 16.2 %slice-start.1 = ((s8[12582912]{0:T(1024)(128)(4,1)}), s8[4194304]{0:T(1024)(128)(4,1)S(1)}, s32[]{:S(2)}) async-start(s8[12582912]{0:T(1024)(128)(4,1)} %bitcast.235), calls=%async_computation.5 | async-start | bytes 8388608
  168.0 9.8 %slice-start.2 = ((s8[12582912]{0:T(1024)(128)(4,1)}), s8[4194304]{0:T(1024)(128)(4,1)S(1)}, s32[]{:S(2)}) async-start(s8[12582912]{0:T(1024)(128)(4,1)} %bitcast.235), calls=%async_computation.6 | async-start | bytes 8388608
  185.0 18.7 %copy-start.26 = (bf16[1024,384]{0,1:T(8,128)(2,1)S(1)}, bf16[1024,384]{0,1:T(8,128)(2,1)}, u32[]{:S(2)}) copy-start(bf16[1024,384]{0,1:T(8,128)(2,1)} %copy-done.25) | copy-start | bytes 2359300
  203.8 5.1 %copy-start.10 = (bf16[6,512,1024]{2,1,0:T(8,128)(2,1)S(1)}, bf16[6,512,1024]{2,1,0:T(8,128)(2,1)}, u32[]{:S(2)}) copy-start(bf16[6,512,1024]{2,1,0:T(8,128)(2,1)} %get-tuple-element.391) | copy-start | bytes 18874372
  208.9 6.9 %slice-start.11 = ((s8[6291456]{0:T(1024)(128)(4,1)}), s8[4194304]{0:T(1024)(128)(4,1)S(1)}, s32[]{:S(2)}) async-start(s8[6291456]{0:T(1024)(128)(4,1)} %bitcast.245), calls=%async_computation.15 | async-start | bytes 8388608
  210.1 5.6 %slice-start.12 = ((s8[6291456]{0:T(1024)(128)(4,1)}), s8[2097152]{0:T(1024)(128)(4,1)S(1)}, s32[]{:S(2)}) async-start(s8[6291456]{0:T(1024)(128)(4,1)} %bitcast.245), calls=%async_computation.16 | async-start | bytes 4194304
  219.1 7.6 %copy-start.51 = (bf16[6,64,1024]{2,1,0:T(8,128)(2,1)}, bf16[6,64,1024]{2,1,0:T(8,128)(2,1)S(1)}, u32[]{:S(2)}) copy-start(bf16[6,64,1024]{2,1,0:T(8,128)(2,1)S(1)} %add_convert_fusion.5) | copy-start | bytes 2359300
  221.3 9.4 %collective-permute-start.7 = (bf16[512,768]{0,1:T(8,128)(2,1)}, bf16[512,768]{0,1:T(8,128)(2,1)}, u32[]{:S(2)}, u32[]{:S(2)}) collective-permute-start(bf16[512,768]{0,1:T(8,128)(2,1)} %broadcast_select_fusion.4), channel_id=1, source_target_pairs={{0,1},{1,0},{2,3},{3,2},{4,5},{5,4},{6,7},{7,6},{8,9},{9,8},{10,11... | collective-permute-start | bytes 2359304 | tf_op jit(solution)/shard_map/ppermute | solution.py:158
  236.1 12.9 %collective-permute-start.8 = (bf16[512,768]{0,1:T(8,128)(2,1)S(1)}, bf16[512,768]{0,1:T(8,128)(2,1)}, u32[]{:S(2)}, u32[]{:S(2)}) collective-permute-start(bf16[512,768]{0,1:T(8,128)(2,1)S(1)} %add_convert_fusion.9), channel_id=1, source_target_pairs={{0,1},{1,0},{2,3},{3,2},{4,5},{5,4},{6,7},{7,6},{8,9},{9,8},{10,11... | collective-permute-start | bytes 2359304 | tf_op jit(solution)/shard_map/ppermute | solution.py:158
  236.8 11.0 %collective-permute-start.11 = (f32[3072]{0:T(1024)S(1)}, f32[3072]{0:T(1024)S(1)}, u32[]{:S(2)}, u32[]{:S(2)}) collective-permute-start(f32[3072]{0:T(1024)S(1)} %pad_maximum_fusion.16), channel_id=1, source_target_pairs={{0,1},{1,0},{2,3},{3,2},{4,5},{5,4},{6,7},{7,6},{8,9},{9,8},{10,11... | collective-permute-start | bytes 36872 | tf_op jit(solution)/shard_map/ppermute | solution.py:158
  240.4 8.7 %copy-start.18 = (f32[512,768]{0,1:T(8,128)S(1)}, f32[512,768]{0,1:T(8,128)}, u32[]{:S(2)}) copy-start(f32[512,768]{0,1:T(8,128)} %copy-done.17) | copy-start | bytes 4718596
  240.4 8.7 %copy-start.142 = (f32[512]{0:T(512)S(1)}, f32[512]{0:T(512)}, u32[]{:S(2)}) copy-start(f32[512]{0:T(512)} %copy-done.141) | copy-start | bytes 6148
  240.4 80.0 %all-to-all-start.1 = ((bf16[16,48,1536]{2,1,0:T(8,128)(2,1)}), bf16[16,48,1536]{2,1,0:T(8,128)(2,1)}, u32[]{:S(2)}, u32[]{:S(2)}) async-start(bf16[16,48,1536]{2,1,0:T(8,128)(2,1)} %bitcast.255), calls=%async_computation.1 | async-start | bytes 4718592 | tf_op jit(solution)/shard_map/all_to_all | solution.py:323
  253.8 7.2 %slice-start.7 = ((s8[4718592]{0:T(1024)(128)(4,1)}), s8[4194304]{0:T(1024)(128)(4,1)S(1)}, s32[]{:S(2)}) async-start(s8[4718592]{0:T(1024)(128)(4,1)} %bitcast.241), calls=%async_computation.11 | async-start | bytes 8388608
  261.0 6.1 %slice-start.3 = ((s8[6291456]{0:T(1024)(128)(4,1)}), s8[4194304]{0:T(1024)(128)(4,1)S(1)}, s32[]{:S(2)}) async-start(s8[6291456]{0:T(1024)(128)(4,1)} %bitcast.237), calls=%async_computation.7 | async-start | bytes 8388608
  261.2 5.9 %slice-start.4 = ((s8[6291456]{0:T(1024)(128)(4,1)}), s8[2097152]{0:T(1024)(128)(4,1)S(1)}, s32[]{:S(2)}) async-start(s8[6291456]{0:T(1024)(128)(4,1)} %bitcast.237), calls=%async_computation.8 | async-start | bytes 4194304
  274.5 7.1 %copy-start.54 = (bf16[512,384]{0,1:T(8,128)(2,1)S(1)}, bf16[512,384]{0,1:T(8,128)(2,1)}, u32[]{:S(2)}) copy-start(bf16[512,384]{0,1:T(8,128)(2,1)} %copy-done.53) | copy-start | bytes 1179652
  278.0 8.9 %slice-start.13 = ((s8[6291456]{0:T(1024)(128)(4,1)}), s8[4194304]{0:T(1024)(128)(4,1)S(1)}, s32[]{:S(2)}) async-start(s8[6291456]{0:T(1024)(128)(4,1)} %bitcast.247), calls=%async_computation.17 | async-start | bytes 8388608
  282.2 8.6 %copy-start.77 = (bf16[6,64,256]{2,1,0:T(8,128)(2,1)}, bf16[6,64,256]{2,1,0:T(8,128)(2,1)S(1)}, u32[]{:S(2)}) copy-start(bf16[6,64,256]{2,1,0:T(8,128)(2,1)S(1)} %convolution_convert_fusion.21) | copy-start | bytes 589828
  282.3 5.1 %slice-start.6 = ((s8[6291456]{0:T(1024)(128)(4,1)}), s8[2097152]{0:T(1024)(128)(4,1)S(1)}, s32[]{:S(2)}) async-start(s8[6291456]{0:T(1024)(128)(4,1)} %bitcast.239), calls=%async_computation.10 | async-start | bytes 4194304
  282.3 5.7 %slice-start.14 = ((s8[6291456]{0:T(1024)(128)(4,1)}), s8[2097152]{0:T(1024)(128)(4,1)S(1)}, s32[]{:S(2)}) async-start(s8[6291456]{0:T(1024)(128)(4,1)} %bitcast.247), calls=%async_computation.18 | async-start | bytes 4194304
  295.5 5.4 %copy-start.149 = (f32[1,1536]{1,0:T(1,128)S(1)}, f32[1,1536]{1,0:T(1,128)}, u32[]{:S(2)}) copy-start(f32[1,1536]{1,0:T(1,128)} %stack.28) | copy-start | bytes 18436
  295.5 5.4 %copy-start.150 = (f32[1,1536]{1,0:T(1,128)S(1)}, f32[1,1536]{1,0:T(1,128)}, u32[]{:S(2)}) copy-start(f32[1,1536]{1,0:T(1,128)} %stack.29) | copy-start | bytes 18436
  295.5 6.9 %copy-start.35 = (bf16[512,768]{0,1:T(8,128)(2,1)S(1)}, bf16[512,768]{0,1:T(8,128)(2,1)}, u32[]{:S(2)}) copy-start(bf16[512,768]{0,1:T(8,128)(2,1)} %copy-done.34) | copy-start | bytes 2359300
  295.5 6.9 %copy-start.37 = (bf16[512,768]{0,1:T(8,128)(2,1)S(1)}, bf16[512,768]{0,1:T(8,128)(2,1)}, u32[]{:S(2)}) copy-start(bf16[512,768]{0,1:T(8,128)(2,1)} %copy-done.36) | copy-start | bytes 2359300
  306.6 19.7 %copy-start.52 = (bf16[6,64,1024]{2,1,0:T(8,128)(2,1)S(1)}, bf16[6,64,1024]{2,1,0:T(8,128)(2,1)}, u32[]{:S(2)}) copy-start(bf16[6,64,1024]{2,1,0:T(8,128)(2,1)} %copy-done.51) | copy-start | bytes 2359300
  306.6 19.7 %copy-start.107 = (bf16[768,384]{1,0:T(8,128)(2,1)S(1)}, bf16[768,384]{1,0:T(8,128)(2,1)}, u32[]{:S(2)}) copy-start(bf16[768,384]{1,0:T(8,128)(2,1)} %param.77) | copy-start | bytes 1769476
  320.3 75.7 %all-to-all-start = ((bf16[16,62,1536]{2,1,0:T(8,128)(2,1)}), bf16[16,62,1536]{2,1,0:T(8,128)(2,1)}, u32[]{:S(2)}, u32[]{:S(2)}) async-start(bf16[16,62,1536]{2,1,0:T(8,128)(2,1)} %pad_maximum_fusion.1), calls=%async_computation | async-start | bytes 6291456 | tf_op jit(solution)/shard_map/all_to_all | solution.py:323
  329.7 7.1 %collective-permute-start.10 = (bf16[512,768]{0,1:T(8,128)(2,1)}, bf16[512,768]{0,1:T(8,128)(2,1)}, u32[]{:S(2)}, u32[]{:S(2)}) collective-permute-start(bf16[512,768]{0,1:T(8,128)(2,1)} %broadcast_select_fusion), channel_id=1, source_target_pairs={{0,1},{1,0},{2,3},{3,2},{4,5},{5,4},{6,7},{7,6},{8,9},{9,8},{10,11... | collective-permute-start | bytes 2359304 | tf_op jit(solution)/shard_map/ppermute | solution.py:158
  333.2 9.9 %collective-permute-start.9 = (bf16[512,768]{0,1:T(8,128)(2,1)S(1)}, bf16[512,768]{0,1:T(8,128)(2,1)S(1)}, u32[]{:S(2)}, u32[]{:S(2)}) collective-permute-start(bf16[512,768]{0,1:T(8,128)(2,1)S(1)} %broadcast_select_fusion.1), channel_id=1, source_target_pairs={{0,1},{1,0},{2,3},{3,2},{4,5},{5,4},{6,7},{7,6},{8,9},{9,8},{10,11... | collective-permute-start | bytes 2359304 | tf_op jit(solution)/shard_map/ppermute | solution.py:158
  336.8 6.2 %copy-start.19 = (f32[512,768]{0,1:T(8,128)S(1)}, f32[512,768]{0,1:T(8,128)}, u32[]{:S(2)}) copy-start(f32[512,768]{0,1:T(8,128)} %copy-done.17) | copy-start | bytes 4718596
  336.8 6.2 %copy-start.143 = (f32[512]{0:T(512)S(1)}, f32[512]{0:T(512)}, u32[]{:S(2)}) copy-start(f32[512]{0:T(512)} %copy-done.141) | copy-start | bytes 6148
  351.2 53.2 %copy-start.1 = (bf16[768,1536]{1,0:T(8,128)(2,1)S(1)}, bf16[768,1536]{1,0:T(8,128)(2,1)}, u32[]{:S(2)}) copy-start(bf16[768,1536]{1,0:T(8,128)(2,1)} %param.88) | copy-start | bytes 7077892
  (155 other events, 362.2 us)
Sparse Core Ops, SparseCore 0:
  157.8 163.1 reduce-scatter.1
